TPU v7x, 32 devices: a whole 2x2x4 slice. The times are simulated.
32 devices in a mesh: gx: 8 (over z, x), gz: 4 (over y, core).
Axes of the slice: x: 2, y: 2, z: 4, core: 2. Of those that a mesh axis runs over, the one named last changes fastest.
Arguments:
- velocity: float32 [3, 64, 128, 384], P(None, 'gx', 'gz'), may hold values from -6 to 6
- y_gap: float32 [385], replicated, may hold values from 0.2 to 2
Outputs:
- eddy_visc: float32 [64, 128, 384], P('gx', 'gz')
- lm_field: float32 [64, 128, 384], P('gx', 'gz')
- mm_field: float32 [64, 128, 384], P('gx', 'gz')
- coefficient: float32 [384], replicated
All inputs are finite; a program needn't handle non-finite values.
Results may differ from a plain program's by a relative error of at most 0.00002.
Values sent between devices are 32-bit elements; how exact they have to be, the bound alone decides.
A program may use at most 64 MiB of HBM per device.

v0:
```python
import functools

import jax
import jax.numpy as jnp
from jax import lax
from jax.experimental import pallas as pl
from jax.experimental.pallas import tpu as pltpu
from jax.sharding import PartitionSpec as P

MESH = pl.DeviceIdType.MESH
LANES = 128
RIM = 8


def width_square(span):
    return jnp.exp(jnp.log(0.5 * span) * (2.0 / 3.0))


def finish(size_ref, lm_ref, mm_ref, coef_ref, eddy_out, lm_out, mm_out, coef_out, eddy_s, sem):
    nx, _, ny = size_ref.shape
    copies = [pltpu.make_async_copy(lm_ref, lm_out, sem.at[0]), pltpu.make_async_copy(mm_ref, mm_out, sem.at[1])]
    for copy in copies:
        copy.start()
    factor = coef_ref[1:2]
    for r in range(0, nx, 2):
        rows = pl.ds(r, 2)
        eddy_s[rows] = factor * size_ref[rows]
        copy = pltpu.make_async_copy(eddy_s.at[rows], eddy_out.at[rows], sem.at[2 + r // 2])
        copy.start()
        copies.append(copy)
    coef_out[...] = coef_ref[0:1].reshape(ny)
    for copy in copies:
        copy.wait()


def kernel(gxn, gzn, cells, gap_hbm, vel_ref, size_s, lm_s, mm_s, out_coef_ref,
           pad, zvel, zpair, zstress, slope, tslope, coef_ref, sums, acc_z, acc_x,
           gap_ref, gap_sem, local_sem, xs_sem, xr_sem, ks_sem, kr_sem, cs_sem, cr_sem,
           zs_sem, zr_sem, ws_sem, wr_sem):
    gx, gz = lax.axis_index("gx"), lax.axis_index("gz")
    nx, nz, ny = vel_ref.shape[1:]
    wide = nz + RIM
    right, left = lax.rem(gx + 1, gxn), lax.rem(gx + gxn - 1, gxn)
    after, before = lax.rem(gz + 1, gzn), lax.rem(gz + gzn - 1, gzn)

    load = pltpu.make_async_copy(vel_ref, pad.at[:, 2:nx + 2, 0:nz], local_sem)
    load.start()
    gap_load = pltpu.make_async_copy(gap_hbm, gap_ref, gap_sem)
    gap_load.start()
    barrier = pltpu.get_barrier_semaphore()
    for d in range(1, gxn):
        pl.semaphore_signal(barrier, inc=1, device_id=(lax.rem(gx + d, gxn), gz), device_id_type=MESH)
    for d in range(1, gzn):
        pl.semaphore_signal(barrier, inc=1, device_id=(gx, lax.rem(gz + d, gzn)), device_id_type=MESH)
    sums[...] = jnp.zeros_like(sums)
    gap_load.wait()
    span = gap_ref[:, 0:ny] + gap_ref[:, 1:ny + 1]
    at = lax.broadcasted_iota(jnp.int32, (1, ny), 1)
    width_sq = width_square(span)
    inverse = 2.0 / span
    coef_ref[0:1] = jnp.where(at == ny - 1, 0.0, inverse)
    coef_ref[1:2] = jnp.where(at == 0, 0.0, inverse)
    coef_ref[2:3] = width_sq * (1.0 / 256.0)
    coef_ref[3:4] = width_sq * width_sq * (1.0 / 256.0)
    coef_ref[4:5] = width_sq
    load.wait()
    pl.semaphore_wait(barrier, gxn + gzn - 2)

    def remote(src, dst, send, recv, device):
        return pltpu.make_async_remote_copy(
            src_ref=src, dst_ref=dst, send_sem=send, recv_sem=recv,
            device_id=device, device_id_type=MESH)

    pieces = ((slice(0, 2), 0, 8), (slice(0, 2), nz - 8, 8), (slice(1, 2), 8, nz - 16), (slice(0, 1), 8, nz - 16))
    x_copies = []
    for n, (layers, start, count) in enumerate(pieces):
        ks = pl.ds(start, count)
        low, high = layers.start, 2 - layers.stop
        deep = layers.stop - layers.start
        x_copies.append((
            remote(pad.at[:, nx + low:nx + low + deep, ks], pad.at[:, low:low + deep, ks], xs_sem.at[n, 0], xr_sem.at[n, 0], (right, gz)),
            remote(pad.at[:, 2 + high:2 + high + deep, ks], pad.at[:, nx + 2 + high:nx + 2 + high + deep, ks], xs_sem.at[n, 1], xr_sem.at[n, 1], (left, gz))))
    k_up = remote(pad.at[:, 2:nx + 2, nz - 2:nz], pad.at[:, 2:nx + 2, wide - 2:wide], ks_sem.at[0], kr_sem.at[0], (gx, after))
    k_down = remote(pad.at[:, 2:nx + 2, 0:2], pad.at[:, 2:nx + 2, nz:nz + 2], ks_sem.at[1], kr_sem.at[1], (gx, before))
    k_up.start()
    k_down.start()
    for pair in x_copies:
        for copy in pair:
            copy.start()

    half_ahead, half_back = coef_ref[0:1, :], coef_ref[1:2, :]

    def filtered(f):
        twice = f + pltpu.roll(f, 1, 0)
        return twice + pltpu.roll(twice, wide - 1, 0)

    def lane_slope(f):
        return pltpu.roll(f, ny - 1, 1) * half_ahead - pltpu.roll(f, 1, 1) * half_back

    def tiles():
        return [pl.ds(t, LANES) for t in range(0, ny, LANES)]

    def smooth_row(r):
        for c in range(3):
            for cols in tiles():
                zvel[c, r, :, cols] = filtered(pad[c, r, :, cols])

    def first(r, inside=True):
        for c in range(3):
            slope[c] = lane_slope(pad[c, r])
        for cols in tiles():
            u = [pad[c, r, :, cols] for c in range(3)]
            a = [pad[c, r + 1, :, cols] - pad[c, r - 1, :, cols] for c in range(3)]
            b = []
            for c in range(3):
                prev, nxt = pltpu.roll(u[c], 1, 0), pltpu.roll(u[c], wide - 1, 0)
                b.append(nxt - prev)
                zvel[c, r, :, cols] = (nxt + prev) + 2.0 * u[c]
            d = [slope[c, :, cols] for c in range(3)]
            strain = [a[0], d[1], b[2], d[0] + a[1], b[0] + a[2], b[1] + d[2]]
            square = [s * s for s in strain]
            size = jnp.sqrt(0.5 * (square[0] + square[1] + square[2]) + 0.25 * (square[3] + square[4] + square[5]))
            if inside:
                size_s[r - 2, :, cols] = size[:nz]
            for n in range(6):
                zstress[n, r, :, cols] = filtered(size * strain[n])[:nz]
            for n, (i, j) in enumerate(((0, 0), (1, 1), (2, 2), (0, 1), (0, 2), (1, 2))):
                zpair[n, r, :, cols] = filtered(u[i] * u[j])[:nz]

    def second(r):
        for c in range(3):
            v = (zvel[c, r - 1] + zvel[c, r + 1]) + 2.0 * zvel[c, r]
            tslope[c] = v
            slope[c] = lane_slope(v)
        for cols in tiles():
            w = coef_ref[2:3, cols]
            w2 = coef_ref[3:4, cols]
            v_wide = [tslope[c, :, cols] for c in range(3)]
            v = [f[:nz] for f in v_wide]
            a = [(zvel[c, r + 2, 0:nz, cols] - zvel[c, r - 2, 0:nz, cols])
                 + 2.0 * (zvel[c, r + 1, 0:nz, cols] - zvel[c, r - 1, 0:nz, cols]) for c in range(3)]
            b = [(pltpu.roll(f, wide - 1, 0) - pltpu.roll(f, 1, 0))[:nz] for f in v_wide]
            d = [slope[c, 0:nz, cols] for c in range(3)]
            test = [a[0], d[1], b[2], d[0] + a[1], b[0] + a[2], b[1] + d[2]]
            square = [s * s for s in test]
            q = 0.25 * jnp.sqrt(0.5 * (square[0] + square[1] + square[2]) + 0.25 * (square[3] + square[4] + square[5]))
            lm, mm_diag, mm_off = 0.0, 0.0, 0.0
            for n, (i, j) in enumerate(((0, 0), (1, 1), (2, 2), (0, 1), (0, 2), (1, 2))):
                stress = (zstress[n, r - 1, :, cols] + zstress[n, r + 1, :, cols]) + 2.0 * zstress[n, r, :, cols]
                model = stress - q * test[n]
                pair = (zpair[n, r - 1, :, cols] + zpair[n, r + 1, :, cols]) + 2.0 * zpair[n, r, :, cols]
                lm = lm + (pair - v[i] * v[j] * 0.0625) * model
                if n < 3:
                    mm_diag = mm_diag + model * model
                else:
                    mm_off = mm_off + model * model
            lm = lm * w
            mm = (mm_diag + 0.5 * mm_off) * w2
            lm_s[r - 2, :, cols] = lm
            mm_s[r - 2, :, cols] = mm
            for n, f in enumerate((lm, mm)):
                sums[n, :, cols] += jnp.sum(f.reshape(nz // 8, 8, LANES), axis=0)

    def over(lo, hi, body):
        def step(r, carry):
            body(r)
            return carry
        lax.fori_loop(lo, hi, step, 0)

    k_up.wait_recv()
    k_down.wait_recv()
    over(3, nx + 1, first)
    smooth_row(2)
    smooth_row(nx + 1)
    over(4, nx, second)

    def both(low, high, body):
        def step(n, carry):
            body(lax.select(n == 0, low, high))
            return carry
        lax.fori_loop(0, 2, step, 0)

    for n in (0, 1):
        for copy in x_copies[n]:
            copy.wait_recv()
    corners = []
    for n, rows in enumerate((slice(0, 2), slice(nx + 2, nx + 4))):
        corners.append(remote(pad.at[:, rows, nz - 2:nz], pad.at[:, rows, wide - 2:wide], cs_sem.at[n, 0], cr_sem.at[n, 0], (gx, after)))
        corners.append(remote(pad.at[:, rows, 0:2], pad.at[:, rows, nz:nz + 2], cs_sem.at[n, 1], cr_sem.at[n, 1], (gx, before)))
    for copy in corners:
        copy.start()
    for copy in x_copies[2]:
        copy.wait_recv()
    for copy in corners:
        copy.wait_recv()
    both(2, nx + 1, first)
    both(1, nx + 2, smooth_row)
    both(3, nx, second)
    for copy in x_copies[3]:
        copy.wait_recv()
    both(1, nx + 2, functools.partial(first, inside=False))
    both(0, nx + 3, smooth_row)
    both(2, nx + 1, second)

    def exchange(acc, me, size, send, recv, device):
        copies = []
        for d in range(1, size):
            there = lax.rem(me + d, size)
            copy = remote(acc.at[me], acc.at[me], send.at[d - 1], recv.at[d - 1], device(there))
            copy.start()
            copies.append(copy)
        return copies

    def collect(acc, me, size, send, recv, device):
        for d in range(1, size):
            source = lax.rem(me + size - d, size)
            remote(acc.at[source], acc.at[source], send.at[d - 1], recv.at[d - 1], device(source)).wait_recv()
        total = acc[0]
        for n in range(1, size):
            total = total + acc[n]
        return total

    z_args = (acc_z, gz, gzn, zs_sem, zr_sem, lambda other: (gx, other))
    x_args = (acc_x, gx, gxn, ws_sem, wr_sem, lambda other: (other, gz))
    acc_z[gz] = jnp.sum(sums[...], axis=1)
    z_copies = exchange(*z_args)
    acc_x[gx] = collect(*z_args)
    w_copies = exchange(*x_args)
    total = collect(*x_args)
    coefficient = total[0:1] / cells / (total[1:2] / cells + 1e-06)
    out_coef_ref[0:1] = coefficient
    out_coef_ref[1:2] = coefficient * coef_ref[4:5]
    k_up.wait_send()
    k_down.wait_send()
    for pair in x_copies:
        for copy in pair:
            copy.wait_send()
    for copy in corners + z_copies + w_copies:
        copy.wait_send()


def per_device(velocity, y_gap):
    gxn, gzn = lax.axis_size("gx"), lax.axis_size("gz")
    _, nx, nz, ny = velocity.shape
    cells = float(nx * gxn * nz * gzn)
    field = jax.ShapeDtypeStruct((nx, nz, ny), jnp.float32)
    f32 = jnp.float32
    wide = nz + RIM
    dma = pltpu.SemaphoreType.DMA
    gaps = y_gap.reshape(1, ny + 1)
    near = pl.BlockSpec(memory_space=pltpu.VMEM)
    far = pl.BlockSpec(memory_space=pl.ANY)
    held = pltpu.VMEM((nx, nz, ny), f32)
    size, lm, mm, coefficient = pl.pallas_call(
        functools.partial(kernel, gxn, gzn, cells),
        out_shape=(held, held, held, pltpu.VMEM((2, ny), f32)),
        in_specs=[far, far],
        out_specs=(near,) * 4,
        scratch_shapes=[
            pltpu.VMEM((3, nx + 4, wide, ny), f32),
            pltpu.VMEM((3, nx + 4, wide, ny), f32),
            pltpu.VMEM((6, nx + 4, nz, ny), f32),
            pltpu.VMEM((6, nx + 4, nz, ny), f32),
            pltpu.VMEM((3, wide, ny), f32),
            pltpu.VMEM((3, wide, ny), f32),
            pltpu.VMEM((8, ny), f32),
            pltpu.VMEM((2, 8, ny), f32),
            pltpu.VMEM((gzn, 2, ny), f32),
            pltpu.VMEM((gxn, 2, ny), f32),
            pltpu.VMEM((1, ny + 1), f32), dma,
            dma, dma((4, 2)), dma((4, 2)), dma((2,)), dma((2,)), dma((2, 2)), dma((2, 2)),
            dma((max(gzn - 1, 1),)), dma((max(gzn - 1, 1),)), dma((max(gxn - 1, 1),)), dma((max(gxn - 1, 1),)),
        ],
        compiler_params=pltpu.CompilerParams(
            collective_id=0, has_side_effects=True, vmem_limit_bytes=40 * 2**20),
    )(pltpu.with_memory_space_constraint(gaps, pltpu.HBM), pltpu.with_memory_space_constraint(velocity, pltpu.HBM))
    return pl.pallas_call(
        finish,
        out_shape=(field, field, field, jax.ShapeDtypeStruct((ny,), f32)),
        in_specs=[near] * 4,
        out_specs=(far, far, far, near),
        scratch_shapes=[pltpu.VMEM((nx, nz, ny), f32), dma((2 + (nx + 1) // 2,))],
        compiler_params=pltpu.CompilerParams(vmem_limit_bytes=8 * 2**20),
    )(size, lm, mm, coefficient)


def solution(mesh):
    placed = (P(None, "gx", "gz", None), P())
    return jax.shard_map(
        per_device,
        mesh=mesh,
        in_specs=placed,
        out_specs=(P("gx", "gz", None), P("gx", "gz", None), P("gx", "gz", None), P()),
        check_vma=False,
    )
```

profile of v0, /device:TPU:0, one launch (start us, length us, event | category | flops | bytes accessed | tf_op | source)
XLA Modules:
  0.0 31.2 jit_solution(7617022002490845795)
XLA Ops:
  0.6 29.0 %shard_map.57 = (f32[8,32,384]{2,1,0:T(8,128)S(1)}, f32[8,32,384]{2,1,0:T(8,128)S(1)}, f32[8,32,384]{2,1,0:T(8,128)S(1)}, f32[2,384]{1,0:T(2,128)S(1)}) custom-call(f32[1,385]{1,0:T(1,128)} %bitcast.1, f32[3,8,32,384]{3,2,1,0:T(8,128)} %vel_ref.1), custom_call_target="tpu_custom_call" | custom-call | tf_op jit(solution)/shard_map/pallas_call | solution.py:254
  29.6 1.6 %shard_map.58 = (f32[8,32,384]{2,1,0:T(8,128)}, f32[8,32,384]{2,1,0:T(8,128)}, f32[8,32,384]{2,1,0:T(8,128)}, f32[384]{0:T(512)}) custom-call(f32[8,32,384]{2,1,0:T(8,128)S(1)} %get-tuple-element.8.size_ref, f32[8,32,384]{2,1,0:T(8,128)S(1)} %get-tuple-element.9.lm_ref, f32[8,32,384]{2,1,0:T(8,128)S(1)} %get-tuple-element.10.mm_ref, ...), custom_call_target="tpu_custom_call" | custom-call | tf_op jit(solution)/shard_map/pallas_call | solution.py:277
where the time goes:
time: 31.4 us; the launch traced here: 31.2 us
  Pallas kernels  30.6 us (97%)
  between operations  0.64 us (2%)
    pallas_call x1, Pallas kernels, per_device(): pl.pallas_call(functools.partial(kernel, gxn, gzn, cells), out_shape=(hel...  29 us
    pallas_call x1, Pallas kernels, per_device(): pl.pallas_call(finish, out_shape=(field, field, field, jax.ShapeDtypeStru...  1.61 us

commit v1 on v0

v1 whole, which is shorter than its diff:
```python
import functools

import jax
import jax.numpy as jnp
from jax import lax
from jax.experimental import pallas as pl
from jax.experimental.pallas import tpu as pltpu
from jax.sharding import PartitionSpec as P

MESH = pl.DeviceIdType.MESH
LANES = 128
RIM = 8
DIRECT = 64


def width_square(span):
    return jnp.exp(jnp.log(0.5 * span) * (2.0 / 3.0))


def finish(size_ref, lm_ref, mm_ref, coef_ref, eddy_out, lm_out, mm_out, coef_out, eddy_s, sem):
    nx, _, ny = size_ref.shape
    copies = [pltpu.make_async_copy(lm_ref, lm_out, sem.at[0]), pltpu.make_async_copy(mm_ref, mm_out, sem.at[1])]
    for copy in copies:
        copy.start()
    factor = coef_ref[1:2]
    for r in range(0, nx, 2):
        rows = pl.ds(r, 2)
        eddy_s[rows] = factor * size_ref[rows]
        copy = pltpu.make_async_copy(eddy_s.at[rows], eddy_out.at[rows], sem.at[2 + r // 2])
        copy.start()
        copies.append(copy)
    coef_out[...] = coef_ref[0:1].reshape(ny)
    for copy in copies:
        copy.wait()


def doublings(size):
    reach, steps = 1, []
    while reach < size // 2:
        steps.append(reach)
        reach *= 2
    return steps


def kernel(gxn, gzn, cells, gap_hbm, vel_ref, size_s, lm_s, mm_s, out_coef_ref,
           pad, zvel, zpair, zstress, slope, tslope, vslope, coef_ref, sums, accs,
           gap_ref, gap_sem, load_sem, xs_sem, xr_sem, ks_sem, kr_sem, cs_sem, cr_sem,
           near_x, near_z, near_all, as_sem, ar_sem):
    gx, gz = lax.axis_index("gx"), lax.axis_index("gz")
    nx, nz, ny = vel_ref.shape[1:]
    wide = nz + RIM
    tiles = [pl.ds(t, LANES) for t in range(0, ny, LANES)]

    def along_x(d):
        return (lax.rem(gx + d + gxn, gxn), gz)

    def along_z(d):
        return (gx, lax.rem(gz + d + gzn, gzn))

    def signal(sem, device):
        pl.semaphore_signal(sem, inc=1, device_id=device, device_id_type=MESH)

    def remote(src, dst, send, recv, device):
        return pltpu.make_async_remote_copy(
            src_ref=src, dst_ref=dst, send_sem=send, recv_sem=recv,
            device_id=device, device_id_type=MESH)

    barrier = pltpu.get_barrier_semaphore()
    for device in (along_x(1), along_x(-1), along_z(1), along_z(-1)):
        signal(barrier, device)
    loads = []
    for n, (lo, hi) in enumerate(((0, 2), (nx - 2, nx), (2, nx - 2))):
        loads.append(pltpu.make_async_copy(vel_ref.at[:, lo:hi], pad.at[:, lo + 2:hi + 2, 0:nz], load_sem.at[n]))
    for load in loads:
        load.start()
    gap_load = pltpu.make_async_copy(gap_hbm, gap_ref, gap_sem)
    gap_load.start()

    def side_rows(side):
        def pick(low, high):
            return lax.select(side == 0, low, high)
        return dict(
            inner=pick(3, nx), edge=pick(2, nx + 1), halo=pick(1, nx + 2), far=pick(0, nx + 3),
            to_halo=pick(nx + 2, 1), to_far=pick(nx + 3, 0), near_from=pick(2, nx + 1), far_from=pick(3, nx),
            both_from=pick(2, nx), both_to=pick(nx + 2, 0), both=pick(0, nx + 2))

    parity = lax.rem(gx, 2)
    order = (parity, 1 - parity)
    sides = [side_rows(side) for side in order]
    middle = pl.ds(8, nz - 16)

    def x_pieces(p):
        side, rows = order[p], sides[p]
        device = (lax.select(side == 0, along_x(-1)[0], along_x(1)[0]), gz)
        there = 1 - side
        plan = []
        for ks in (pl.ds(0, 8), pl.ds(nz - 8, 8)):
            plan.append((rows["both_from"], rows["both_to"], rows["both"], 2, ks, pl.ds(0, ny)))
        plan.append((rows["near_from"], rows["to_halo"], rows["halo"], 1, middle, pl.ds(0, ny)))
        for cols in tiles:
            plan.append((rows["far_from"], rows["to_far"], rows["far"], 1, middle, cols))
        out = []
        for n, (src, dst, here, deep, ks, cols) in enumerate(plan):
            send = remote(pad.at[:, pl.ds(src, deep), ks, cols], pad.at[:, pl.ds(dst, deep), ks, cols],
                          xs_sem.at[n, side], xr_sem.at[n, there], device)
            got = pad.at[:, pl.ds(here, deep), ks, cols]
            take = remote(got, got, xs_sem.at[n, side], xr_sem.at[n, side], device)
            out.append((send, take))
        return out

    pieces = [x_pieces(p) for p in range(2)]
    k_up = remote(pad.at[:, 2:nx + 2, nz - 2:nz], pad.at[:, 2:nx + 2, wide - 2:wide], ks_sem.at[0], kr_sem.at[0], along_z(1))
    k_down = remote(pad.at[:, 2:nx + 2, 0:2], pad.at[:, 2:nx + 2, nz:nz + 2], ks_sem.at[1], kr_sem.at[1], along_z(-1))

    for load in loads[:2]:
        load.wait()
    pl.semaphore_wait(barrier, 4)
    for pair in zip(*pieces):
        for send, _ in pair:
            send.start()
    loads[2].wait()
    k_up.start()
    k_down.start()

    know_x, know_z = doublings(gxn), doublings(gzn)
    direct = gxn * gzn <= DIRECT

    def learn_steps():
        last = max(len(know_x), len(know_z))
        for j in range(last + 1):
            if j > 0:
                for sem, steps in ((near_x, know_x), (near_z, know_z)):
                    if j <= len(steps):
                        pl.semaphore_wait(sem.at[j - 1], 2)
            for sem, steps, along in ((near_x, know_x, along_x), (near_z, know_z, along_z)):
                if j < len(steps):
                    signal(sem.at[j], along(steps[j]))
                    signal(sem.at[j], along(-steps[j]))
            if j < last:
                yield
        if direct and gzn > 1:
            for d in range(1, gzn):
                signal(near_all, along_z(d))
            yield
            pl.semaphore_wait(near_all, gzn - 1)

    steps = learn_steps()

    def learn():
        next(steps, None)

    learn()
    sums[...] = jnp.zeros_like(sums)
    gap_load.wait()
    span = gap_ref[:, 0:ny] + gap_ref[:, 1:ny + 1]
    at = lax.broadcasted_iota(jnp.int32, (1, ny), 1)
    width_sq = width_square(span)
    inverse = 2.0 / span
    coef_ref[0:1] = jnp.where(at == ny - 1, 0.0, inverse)
    coef_ref[1:2] = jnp.where(at == 0, 0.0, inverse)
    coef_ref[2:3] = width_sq * (1.0 / 256.0)
    coef_ref[3:4] = width_sq * width_sq * (1.0 / 256.0)
    coef_ref[4:5] = width_sq
    half_ahead, half_back = coef_ref[0:1, :], coef_ref[1:2, :]

    def filtered(f):
        twice = f + pltpu.roll(f, 1, 0)
        return twice + pltpu.roll(twice, wide - 1, 0)

    def lane_slope(f):
        return pltpu.roll(f, ny - 1, 1) * half_ahead - pltpu.roll(f, 1, 1) * half_back

    def smooth_tile(r, cols):
        for c in range(3):
            zvel[c, r, :, cols] = filtered(pad[c, r, :, cols])

    def smooth_row(r):
        for cols in tiles:
            smooth_tile(r, cols)

    def first_slope(r):
        for c in range(3):
            slope[c] = lane_slope(pad[c, r])

    def first_tile(r, cols, inside):
        u = [pad[c, r, :, cols] for c in range(3)]
        a = [pad[c, r + 1, :, cols] - pad[c, r - 1, :, cols] for c in range(3)]
        b = []
        for c in range(3):
            prev, nxt = pltpu.roll(u[c], 1, 0), pltpu.roll(u[c], wide - 1, 0)
            b.append(nxt - prev)
            if inside:
                zvel[c, r, :, cols] = (nxt + prev) + 2.0 * u[c]
        d = [slope[c, :, cols] for c in range(3)]
        strain = [a[0], d[1], b[2], d[0] + a[1], b[0] + a[2], b[1] + d[2]]
        square = [s * s for s in strain]
        size = jnp.sqrt(0.5 * (square[0] + square[1] + square[2]) + 0.25 * (square[3] + square[4] + square[5]))
        if inside:
            size_s[r - 2, :, cols] = size[:nz]
        for n in range(6):
            zstress[n, r, :, cols] = filtered(size * strain[n])[:nz]
        for n, (i, j) in enumerate(((0, 0), (1, 1), (2, 2), (0, 1), (0, 2), (1, 2))):
            zpair[n, r, :, cols] = filtered(u[i] * u[j])[:nz]

    def first(r, inside=True):
        first_slope(r)
        for cols in tiles:
            first_tile(r, cols, inside)

    def second_slope(r):
        for c in range(3):
            v = (zvel[c, r - 1] + zvel[c, r + 1]) + 2.0 * zvel[c, r]
            tslope[c] = v
            vslope[c] = lane_slope(v)

    def second_tile(r, cols):
        w = coef_ref[2:3, cols]
        w2 = coef_ref[3:4, cols]
        v_wide = [tslope[c, :, cols] for c in range(3)]
        v = [f[:nz] for f in v_wide]
        a = [(zvel[c, r + 2, 0:nz, cols] - zvel[c, r - 2, 0:nz, cols])
             + 2.0 * (zvel[c, r + 1, 0:nz, cols] - zvel[c, r - 1, 0:nz, cols]) for c in range(3)]
        b = [(pltpu.roll(f, wide - 1, 0) - pltpu.roll(f, 1, 0))[:nz] for f in v_wide]
        d = [vslope[c, 0:nz, cols] for c in range(3)]
        test = [a[0], d[1], b[2], d[0] + a[1], b[0] + a[2], b[1] + d[2]]
        square = [s * s for s in test]
        q = 0.25 * jnp.sqrt(0.5 * (square[0] + square[1] + square[2]) + 0.25 * (square[3] + square[4] + square[5]))
        lm, mm_diag, mm_off = 0.0, 0.0, 0.0
        for n, (i, j) in enumerate(((0, 0), (1, 1), (2, 2), (0, 1), (0, 2), (1, 2))):
            stress = (zstress[n, r - 1, :, cols] + zstress[n, r + 1, :, cols]) + 2.0 * zstress[n, r, :, cols]
            model = stress - q * test[n]
            pair = (zpair[n, r - 1, :, cols] + zpair[n, r + 1, :, cols]) + 2.0 * zpair[n, r, :, cols]
            lm = lm + (pair - v[i] * v[j] * 0.0625) * model
            if n < 3:
                mm_diag = mm_diag + model * model
            else:
                mm_off = mm_off + model * model
        lm = lm * w
        mm = (mm_diag + 0.5 * mm_off) * w2
        lm_s[r - 2, :, cols] = lm
        mm_s[r - 2, :, cols] = mm
        for n, f in enumerate((lm, mm)):
            sums[n, :, cols] += jnp.sum(f.reshape(nz // 8, 8, LANES), axis=0)

    def second(r):
        second_slope(r)
        for cols in tiles:
            second_tile(r, cols)

    def over(lo, hi, body):
        def step(r, carry):
            body(r)
            return carry
        lax.fori_loop(lo, hi, step, 0)

    k_up.wait_recv()
    k_down.wait_recv()
    learn()
    over(3, nx + 1, first)
    learn()
    smooth_row(2)
    smooth_row(nx + 1)

    def corner_copies(p):
        rows, out = pl.ds(sides[p]["both"], 2), []
        for n, (src, dst, device) in enumerate(((nz - 2, wide - 2, along_z(1)), (0, nz, along_z(-1)))):
            out.append(remote(pad.at[:, rows, pl.ds(src, 2)], pad.at[:, rows, pl.ds(dst, 2)], cs_sem.at[n, order[p]], cr_sem.at[n, order[p]], device))
        return out

    def relay(p):
        for _, take in pieces[p][:2]:
            take.wait_recv()
        for copy in corners[p]:
            copy.start()

    corners = [corner_copies(p) for p in range(2)]
    over(4, nx, second)
    learn()
    relay(0)
    relay(1)

    for _, take in pieces[0][2:]:
        take.wait_recv()
    for copy in corners[0]:
        copy.wait_recv()
    near = sides[0]

    def both(low, high, body):
        def step(n, carry):
            body(lax.select(n == 0, low, high))
            return carry
        lax.fori_loop(0, 2, step, 0)

    first(near["edge"])
    first(near["halo"], False)
    both(near["halo"], near["far"], smooth_row)
    both(near["inner"], near["edge"], second)
    learn()

    last = sides[1]
    pieces[1][2][1].wait_recv()
    for copy in corners[1]:
        copy.wait_recv()
    first(last["edge"])
    smooth_row(last["halo"])
    second(last["inner"])
    first_slope(last["halo"])
    second_slope(last["edge"])
    for cols, (_, take) in zip(tiles, pieces[1][3:]):
        take.wait_recv()
        first_tile(last["halo"], cols, False)
        smooth_tile(last["far"], cols)
        second_tile(last["edge"], cols)

    for _ in steps:
        pass
    total = jnp.sum(sums[...], axis=1)
    if direct:
        rounds = [(gx * gzn + gz, [(lax.rem(gx + dx, gxn), lax.rem(gz + dz, gzn))
                                   for dx in sorted(range(gxn), key=lambda d: -min(d, gxn - d))
                                   for dz in range(gzn) if dx or dz])]
    else:
        rounds = [(gz, [along_z(d) for d in range(1, gzn)]), (gx, [along_x(d) for d in range(1, gxn)])]
    sent = []
    for n, (slot, devices) in enumerate(rounds):
        acc, count = accs[n], len(devices)
        acc[slot] = total
        for device in devices:
            remote(acc.at[slot], acc.at[slot], as_sem.at[n], ar_sem.at[n], device).start()
        every = remote(acc.at[0:count], acc.at[0:count], as_sem.at[n], ar_sem.at[n], (gx, gz))
        every.wait_recv()
        sent.append(every)
        total = jnp.sum(acc[...], axis=0)
    coefficient = total[0:1] / cells / (total[1:2] / cells + 1e-06)
    out_coef_ref[0:1] = coefficient
    out_coef_ref[1:2] = coefficient * coef_ref[4:5]
    k_up.wait_send()
    k_down.wait_send()
    for p in range(2):
        for send, _ in pieces[p]:
            send.wait_send()
        for copy in corners[p]:
            copy.wait_send()
    for copy in sent:
        copy.wait_send()


def per_device(velocity, y_gap):
    gxn, gzn = lax.axis_size("gx"), lax.axis_size("gz")
    _, nx, nz, ny = velocity.shape
    cells = float(nx * gxn * nz * gzn)
    field = jax.ShapeDtypeStruct((nx, nz, ny), jnp.float32)
    f32 = jnp.float32
    wide = nz + RIM
    dma, flag = pltpu.SemaphoreType.DMA, pltpu.SemaphoreType.REGULAR
    members = (gxn * gzn,) if gxn * gzn <= DIRECT else (gzn, gxn)
    parts = 3 + ny // LANES
    gaps = y_gap.reshape(1, ny + 1)
    near = pl.BlockSpec(memory_space=pltpu.VMEM)
    far = pl.BlockSpec(memory_space=pl.ANY)
    held = pltpu.VMEM((nx, nz, ny), f32)
    size, lm, mm, coefficient = pl.pallas_call(
        functools.partial(kernel, gxn, gzn, cells),
        out_shape=(held, held, held, pltpu.VMEM((2, ny), f32)),
        in_specs=[far, far],
        out_specs=(near,) * 4,
        scratch_shapes=[
            pltpu.VMEM((3, nx + 4, wide, ny), f32),
            pltpu.VMEM((3, nx + 4, wide, ny), f32),
            pltpu.VMEM((6, nx + 4, nz, ny), f32),
            pltpu.VMEM((6, nx + 4, nz, ny), f32),
            pltpu.VMEM((3, wide, ny), f32),
            pltpu.VMEM((3, wide, ny), f32),
            pltpu.VMEM((3, wide, ny), f32),
            pltpu.VMEM((8, ny), f32),
            pltpu.VMEM((2, 8, ny), f32),
            tuple(pltpu.VMEM((n, 2, ny), f32) for n in members),
            pltpu.VMEM((1, ny + 1), f32), dma,
            dma((3,)), dma((parts, 2)), dma((parts, 2)), dma((2,)), dma((2,)), dma((2, 2)), dma((2, 2)),
            flag((max(len(doublings(gxn)), 1),)), flag((max(len(doublings(gzn)), 1),)), flag,
            dma((len(members),)), dma((len(members),)),
        ],
        compiler_params=pltpu.CompilerParams(
            collective_id=0, has_side_effects=True, vmem_limit_bytes=40 * 2**20),
    )(pltpu.with_memory_space_constraint(gaps, pltpu.HBM), pltpu.with_memory_space_constraint(velocity, pltpu.HBM))
    return pl.pallas_call(
        finish,
        out_shape=(field, field, field, jax.ShapeDtypeStruct((ny,), f32)),
        in_specs=[near] * 4,
        out_specs=(far, far, far, near),
        scratch_shapes=[pltpu.VMEM((nx, nz, ny), f32), dma((2 + (nx + 1) // 2,))],
        compiler_params=pltpu.CompilerParams(vmem_limit_bytes=8 * 2**20),
    )(size, lm, mm, coefficient)


def solution(mesh):
    placed = (P(None, "gx", "gz", None), P())
    return jax.shard_map(
        per_device,
        mesh=mesh,
        in_specs=placed,
        out_specs=(P("gx", "gz", None), P("gx", "gz", None), P("gx", "gz", None), P()),
        check_vma=False,
    )
```

time: 31.4 us -> 29 us (0.924)
  Pallas kernels: 30.6 us -> 28.3 us
    pallas_call x1, Pallas kernels: 29 us -> 26.6 us  [per_device(): pl.pallas_call(functools.partial(kernel, gxn, gzn, cells), out_shape=(hel...]
where the time goes in v1:
time: 29 us; the launch traced here: 28.9 us
  Pallas kernels  28.3 us (98%)
  between operations  0.64 us (2%)
    pallas_call x1, Pallas kernels, per_device(): pl.pallas_call(functools.partial(kernel, gxn, gzn, cells), out_shape=(hel...  26.6 us
    pallas_call x1, Pallas kernels, per_device(): pl.pallas_call(finish, out_shape=(field, field, field, jax.ShapeDtypeStru...  1.61 us

profile of v1, /device:TPU:0, one launch (start us, length us, event | category | flops | bytes accessed | tf_op | source)
XLA Modules:
  0.0 28.9 jit_solution(556402443475470934)
XLA Ops:
  0.6 26.6 %shard_map.57 = (f32[8,32,384]{2,1,0:T(8,128)S(1)}, f32[8,32,384]{2,1,0:T(8,128)S(1)}, f32[8,32,384]{2,1,0:T(8,128)S(1)}, f32[2,384]{1,0:T(2,128)S(1)}) custom-call(f32[1,385]{1,0:T(1,128)} %bitcast.1, f32[3,8,32,384]{3,2,1,0:T(8,128)} %vel_ref.1), custom_call_target="tpu_custom_call" | custom-call | tf_op jit(solution)/shard_map/pallas_call | solution.py:362
  27.3 1.6 %shard_map.58 = (f32[8,32,384]{2,1,0:T(8,128)}, f32[8,32,384]{2,1,0:T(8,128)}, f32[8,32,384]{2,1,0:T(8,128)}, f32[384]{0:T(512)}) custom-call(f32[8,32,384]{2,1,0:T(8,128)S(1)} %get-tuple-element.8.size_ref, f32[8,32,384]{2,1,0:T(8,128)S(1)} %get-tuple-element.9.lm_ref, f32[8,32,384]{2,1,0:T(8,128)S(1)} %get-tuple-element.10.mm_ref, ...), custom_call_target="tpu_custom_call" | custom-call | tf_op jit(solution)/shard_map/pallas_call | solution.py:386

commit v2 on v1

--- a/solution.py
+++ b/solution.py
@@ -11,6 +11,8 @@
 LANES = 128
 RIM = 8
 DIRECT = 64
+EDGES, NEAR = (0, 1), (2, 3, 4)
+PAIRS = ((0, 0), (1, 1), (2, 2), (0, 1), (0, 2), (1, 2))
 
 
 def width_square(span):
@@ -43,7 +45,7 @@
 
 
 def kernel(gxn, gzn, cells, gap_hbm, vel_ref, size_s, lm_s, mm_s, out_coef_ref,
-           pad, zvel, zpair, zstress, slope, tslope, vslope, coef_ref, sums, accs,
+           pad, zvel, zpair, zstress, slope, tslope, vslope, leon_ref, coef_ref, sums, accs,
            gap_ref, gap_sem, load_sem, xs_sem, xr_sem, ks_sem, kr_sem, cs_sem, cr_sem,
            near_x, near_z, near_all, as_sem, ar_sem):
     gx, gz = lax.axis_index("gx"), lax.axis_index("gz")
@@ -87,37 +89,53 @@
     parity = lax.rem(gx, 2)
     order = (parity, 1 - parity)
     sides = [side_rows(side) for side in order]
-    middle = pl.ds(8, nz - 16)
 
     def x_pieces(p):
         side, rows = order[p], sides[p]
         device = (lax.select(side == 0, along_x(-1)[0], along_x(1)[0]), gz)
         there = 1 - side
         plan = []
-        for ks in (pl.ds(0, 8), pl.ds(nz - 8, 8)):
-            plan.append((rows["both_from"], rows["both_to"], rows["both"], 2, ks, pl.ds(0, ny)))
-        plan.append((rows["near_from"], rows["to_halo"], rows["halo"], 1, middle, pl.ds(0, ny)))
+        both = (2, rows["both_from"], rows["both_to"], rows["both"])
+        near = (1, rows["near_from"], rows["to_halo"], rows["halo"])
+        far = (1, rows["far_from"], rows["to_far"], rows["far"])
+        for ks in (pl.ds(0, 2), pl.ds(nz - 2, 2)):
+            plan.append((both, ks, pl.ds(0, ny)))
+        inner = (pl.ds(2, 6), pl.ds(8, nz - 16), pl.ds(nz - 8, 6))
+        for ks in inner:
+            plan.append((near, ks, pl.ds(0, ny)))
         for cols in tiles:
-            plan.append((rows["far_from"], rows["to_far"], rows["far"], 1, middle, cols))
+            for ks in inner:
+                plan.append((far, ks, cols))
         out = []
-        for n, (src, dst, here, deep, ks, cols) in enumerate(plan):
-            send = remote(pad.at[:, pl.ds(src, deep), ks, cols], pad.at[:, pl.ds(dst, deep), ks, cols],
+        for n, ((deep, src, dst, here), ks, cols) in enumerate(plan):
+            give = remote(pad.at[:, pl.ds(src, deep), ks, cols], pad.at[:, pl.ds(dst, deep), ks, cols],
                           xs_sem.at[n, side], xr_sem.at[n, there], device)
             got = pad.at[:, pl.ds(here, deep), ks, cols]
-            take = remote(got, got, xs_sem.at[n, side], xr_sem.at[n, side], device)
-            out.append((send, take))
+            got = remote(got, got, xs_sem.at[n, side], xr_sem.at[n, side], device)
+            out.append((give, got))
         return out
 
     pieces = [x_pieces(p) for p in range(2)]
     k_up = remote(pad.at[:, 2:nx + 2, nz - 2:nz], pad.at[:, 2:nx + 2, wide - 2:wide], ks_sem.at[0], kr_sem.at[0], along_z(1))
     k_down = remote(pad.at[:, 2:nx + 2, 0:2], pad.at[:, 2:nx + 2, nz:nz + 2], ks_sem.at[1], kr_sem.at[1], along_z(-1))
 
+    def far(t):
+        return tuple(range(5 + 3 * t, 8 + 3 * t))
+
+    def send(*which):
+        for n in which:
+            for p in range(2):
+                pieces[p][n][0].start()
+
+    def take(*which):
+        for n in which:
+            for p in range(2):
+                pieces[p][n][1].wait_recv()
+
     for load in loads[:2]:
         load.wait()
     pl.semaphore_wait(barrier, 4)
-    for pair in zip(*pieces):
-        for send, _ in pair:
-            send.start()
+    send(*EDGES, *NEAR)
     loads[2].wait()
     k_up.start()
     k_down.start()
@@ -178,11 +196,11 @@
         for cols in tiles:
             smooth_tile(r, cols)
 
-    def first_slope(r):
+    def first_slope(r, n=2):
         for c in range(3):
-            slope[c] = lane_slope(pad[c, r])
-
-    def first_tile(r, cols, inside):
+            slope[n, c] = lane_slope(pad[c, r])
+
+    def stress_tile(r, cols, inside, side=2):
         u = [pad[c, r, :, cols] for c in range(3)]
         a = [pad[c, r + 1, :, cols] - pad[c, r - 1, :, cols] for c in range(3)]
         b = []
@@ -191,7 +209,7 @@
             b.append(nxt - prev)
             if inside:
                 zvel[c, r, :, cols] = (nxt + prev) + 2.0 * u[c]
-        d = [slope[c, :, cols] for c in range(3)]
+        d = [slope[side, c, :, cols] for c in range(3)]
         strain = [a[0], d[1], b[2], d[0] + a[1], b[0] + a[2], b[1] + d[2]]
         square = [s * s for s in strain]
         size = jnp.sqrt(0.5 * (square[0] + square[1] + square[2]) + 0.25 * (square[3] + square[4] + square[5]))
@@ -199,38 +217,49 @@
             size_s[r - 2, :, cols] = size[:nz]
         for n in range(6):
             zstress[n, r, :, cols] = filtered(size * strain[n])[:nz]
-        for n, (i, j) in enumerate(((0, 0), (1, 1), (2, 2), (0, 1), (0, 2), (1, 2))):
+
+    def pair_tile(r, cols):
+        u = [pad[c, r, :, cols] for c in range(3)]
+        for n, (i, j) in enumerate(PAIRS):
             zpair[n, r, :, cols] = filtered(u[i] * u[j])[:nz]
 
-    def first(r, inside=True):
+    def first(r):
         first_slope(r)
         for cols in tiles:
-            first_tile(r, cols, inside)
-
-    def second_slope(r):
+            stress_tile(r, cols, True)
+            pair_tile(r, cols)
+
+    def second_slope(r, n=2):
         for c in range(3):
             v = (zvel[c, r - 1] + zvel[c, r + 1]) + 2.0 * zvel[c, r]
-            tslope[c] = v
-            vslope[c] = lane_slope(v)
-
-    def second_tile(r, cols):
+            tslope[n, c] = v
+            vslope[n, c] = lane_slope(v)
+
+    def leonard(r, cols, side=2):
+        v = [tslope[side, c, 0:nz, cols] for c in range(3)]
+        out = []
+        for n, (i, j) in enumerate(PAIRS):
+            pair = (zpair[n, r - 1, :, cols] + zpair[n, r + 1, :, cols]) + 2.0 * zpair[n, r, :, cols]
+            out.append(pair - v[i] * v[j] * 0.0625)
+        return out
+
+    def second_tile(r, cols, side=2, leon=None):
         w = coef_ref[2:3, cols]
         w2 = coef_ref[3:4, cols]
-        v_wide = [tslope[c, :, cols] for c in range(3)]
-        v = [f[:nz] for f in v_wide]
+        v_wide = [tslope[side, c, :, cols] for c in range(3)]
         a = [(zvel[c, r + 2, 0:nz, cols] - zvel[c, r - 2, 0:nz, cols])
              + 2.0 * (zvel[c, r + 1, 0:nz, cols] - zvel[c, r - 1, 0:nz, cols]) for c in range(3)]
         b = [(pltpu.roll(f, wide - 1, 0) - pltpu.roll(f, 1, 0))[:nz] for f in v_wide]
-        d = [vslope[c, 0:nz, cols] for c in range(3)]
+        d = [vslope[side, c, 0:nz, cols] for c in range(3)]
         test = [a[0], d[1], b[2], d[0] + a[1], b[0] + a[2], b[1] + d[2]]
         square = [s * s for s in test]
         q = 0.25 * jnp.sqrt(0.5 * (square[0] + square[1] + square[2]) + 0.25 * (square[3] + square[4] + square[5]))
         lm, mm_diag, mm_off = 0.0, 0.0, 0.0
-        for n, (i, j) in enumerate(((0, 0), (1, 1), (2, 2), (0, 1), (0, 2), (1, 2))):
+        leon = leon or leonard(r, cols, side)
+        for n in range(6):
             stress = (zstress[n, r - 1, :, cols] + zstress[n, r + 1, :, cols]) + 2.0 * zstress[n, r, :, cols]
             model = stress - q * test[n]
-            pair = (zpair[n, r - 1, :, cols] + zpair[n, r + 1, :, cols]) + 2.0 * zpair[n, r, :, cols]
-            lm = lm + (pair - v[i] * v[j] * 0.0625) * model
+            lm = lm + leon[n] * model
             if n < 3:
                 mm_diag = mm_diag + model * model
             else:
@@ -255,93 +284,93 @@
 
     k_up.wait_recv()
     k_down.wait_recv()
-    learn()
     over(3, nx + 1, first)
     learn()
+    take(*EDGES)
+    relayed = []
+    for p in range(2):
+        rows = pl.ds(sides[p]["both"], 2)
+        for n, (src, dst, device) in enumerate(((nz - 2, wide - 2, along_z(1)), (0, nz, along_z(-1)))):
+            relayed.append(remote(pad.at[:, rows, pl.ds(src, 2)], pad.at[:, rows, pl.ds(dst, 2)], cs_sem.at[n, order[p]], cr_sem.at[n, order[p]], device))
+    for copy in relayed:
+        copy.start()
+    send(*far(0))
     smooth_row(2)
     smooth_row(nx + 1)
-
-    def corner_copies(p):
-        rows, out = pl.ds(sides[p]["both"], 2), []
-        for n, (src, dst, device) in enumerate(((nz - 2, wide - 2, along_z(1)), (0, nz, along_z(-1)))):
-            out.append(remote(pad.at[:, rows, pl.ds(src, 2)], pad.at[:, rows, pl.ds(dst, 2)], cs_sem.at[n, order[p]], cr_sem.at[n, order[p]], device))
-        return out
-
-    def relay(p):
-        for _, take in pieces[p][:2]:
-            take.wait_recv()
-        for copy in corners[p]:
-            copy.start()
-
-    corners = [corner_copies(p) for p in range(2)]
     over(4, nx, second)
+    send(*far(1))
+
+    def both(body):
+        for p in range(2):
+            body(p, sides[p])
+
+    take(*NEAR)
+    send(*far(2))
     learn()
-    relay(0)
-    relay(1)
-
-    for _, take in pieces[0][2:]:
-        take.wait_recv()
-    for copy in corners[0]:
+    for copy in relayed:
         copy.wait_recv()
-    near = sides[0]
-
-    def both(low, high, body):
-        def step(n, carry):
-            body(lax.select(n == 0, low, high))
-            return carry
-        lax.fori_loop(0, 2, step, 0)
-
-    first(near["edge"])
-    first(near["halo"], False)
-    both(near["halo"], near["far"], smooth_row)
-    both(near["inner"], near["edge"], second)
-    learn()
-
-    last = sides[1]
-    pieces[1][2][1].wait_recv()
-    for copy in corners[1]:
-        copy.wait_recv()
-    first(last["edge"])
-    smooth_row(last["halo"])
-    second(last["inner"])
-    first_slope(last["halo"])
-    second_slope(last["edge"])
-    for cols, (_, take) in zip(tiles, pieces[1][3:]):
-        take.wait_recv()
-        first_tile(last["halo"], cols, False)
-        smooth_tile(last["far"], cols)
-        second_tile(last["edge"], cols)
-
+
+    def ready(p, rows):
+        first(rows["edge"])
+        smooth_row(rows["halo"])
+        second(rows["inner"])
+        first_slope(rows["halo"], p)
+        second_slope(rows["edge"], p)
+        for cols in tiles:
+            pair_tile(rows["halo"], cols)
+            for n, f in enumerate(leonard(rows["edge"], cols, p)):
+                leon_ref[p, n, :, cols] = f
+
+    ready(0, sides[0])
+    ready(1, sides[1])
     for _ in steps:
         pass
-    total = jnp.sum(sums[...], axis=1)
+    here = gx * gzn + gz
     if direct:
-        rounds = [(gx * gzn + gz, [(lax.rem(gx + dx, gxn), lax.rem(gz + dz, gzn))
-                                   for dx in sorted(range(gxn), key=lambda d: -min(d, gxn - d))
-                                   for dz in range(gzn) if dx or dz])]
+        rounds = [(here, [(lax.rem(gx + dx, gxn), lax.rem(gz + dz, gzn))
+                          for dx in sorted(range(gxn), key=lambda d: -min(d, gxn - d))
+                          for dz in range(gzn) if dx or dz])]
     else:
         rounds = [(gz, [along_z(d) for d in range(1, gzn)]), (gx, [along_x(d) for d in range(1, gxn)])]
-    sent = []
-    for n, (slot, devices) in enumerate(rounds):
-        acc, count = accs[n], len(devices)
-        acc[slot] = total
+
+    def spread(n, t, value):
+        slot, devices = rounds[n]
+        acc = accs[n].at[t]
+        acc[slot] = value
         for device in devices:
-            remote(acc.at[slot], acc.at[slot], as_sem.at[n], ar_sem.at[n], device).start()
-        every = remote(acc.at[0:count], acc.at[0:count], as_sem.at[n], ar_sem.at[n], (gx, gz))
-        every.wait_recv()
-        sent.append(every)
-        total = jnp.sum(acc[...], axis=0)
-    coefficient = total[0:1] / cells / (total[1:2] / cells + 1e-06)
-    out_coef_ref[0:1] = coefficient
-    out_coef_ref[1:2] = coefficient * coef_ref[4:5]
+            remote(acc.at[slot], acc.at[slot], as_sem.at[n, t], ar_sem.at[n, t], device).start()
+
+    def gathered(n, t):
+        acc, count = accs[n].at[t], len(rounds[n][1])
+        return remote(acc.at[0:count], acc.at[0:count], as_sem.at[n, t], ar_sem.at[n, t], (gx, gz))
+
+    for t, cols in enumerate(tiles):
+        take(*far(t))
+
+        def finish_rows(p, rows):
+            stress_tile(rows["halo"], cols, False, p)
+            smooth_tile(rows["far"], cols)
+            second_tile(rows["edge"], cols, p, [leon_ref[p, n, :, cols] for n in range(6)])
+
+        both(finish_rows)
+        spread(0, t, jnp.sum(sums[:, :, cols], axis=1))
+    for n in range(1, len(rounds) + 1):
+        for t, cols in enumerate(tiles):
+            gathered(n - 1, t).wait_recv()
+            total = jnp.sum(accs[n - 1][t], axis=0)
+            if n < len(rounds):
+                spread(n, t, total)
+            else:
+                coefficient = total[0:1] / cells / (total[1:2] / cells + 1e-06)
+                out_coef_ref[0:1, cols] = coefficient
+                out_coef_ref[1:2, cols] = coefficient * coef_ref[4:5, cols]
+    sent = [gathered(n, t) for n in range(len(rounds)) for t in range(len(tiles))]
     k_up.wait_send()
     k_down.wait_send()
     for p in range(2):
-        for send, _ in pieces[p]:
-            send.wait_send()
-        for copy in corners[p]:
+        for copy, _ in pieces[p]:
             copy.wait_send()
-    for copy in sent:
+    for copy in relayed + sent:
         copy.wait_send()
 
 
@@ -354,7 +383,7 @@
     wide = nz + RIM
     dma, flag = pltpu.SemaphoreType.DMA, pltpu.SemaphoreType.REGULAR
     members = (gxn * gzn,) if gxn * gzn <= DIRECT else (gzn, gxn)
-    parts = 3 + ny // LANES
+    parts = 5 + 3 * (ny // LANES)
     gaps = y_gap.reshape(1, ny + 1)
     near = pl.BlockSpec(memory_space=pltpu.VMEM)
     far = pl.BlockSpec(memory_space=pl.ANY)
@@ -369,16 +398,17 @@
             pltpu.VMEM((3, nx + 4, wide, ny), f32),
             pltpu.VMEM((6, nx + 4, nz, ny), f32),
             pltpu.VMEM((6, nx + 4, nz, ny), f32),
-            pltpu.VMEM((3, wide, ny), f32),
-            pltpu.VMEM((3, wide, ny), f32),
-            pltpu.VMEM((3, wide, ny), f32),
+            pltpu.VMEM((3, 3, wide, ny), f32),
+            pltpu.VMEM((3, 3, wide, ny), f32),
+            pltpu.VMEM((3, 3, wide, ny), f32),
+            pltpu.VMEM((2, 6, nz, ny), f32),
             pltpu.VMEM((8, ny), f32),
             pltpu.VMEM((2, 8, ny), f32),
-            tuple(pltpu.VMEM((n, 2, ny), f32) for n in members),
+            tuple(pltpu.VMEM((ny // LANES, n, 2, LANES), f32) for n in members),
             pltpu.VMEM((1, ny + 1), f32), dma,
             dma((3,)), dma((parts, 2)), dma((parts, 2)), dma((2,)), dma((2,)), dma((2, 2)), dma((2, 2)),
             flag((max(len(doublings(gxn)), 1),)), flag((max(len(doublings(gzn)), 1),)), flag,
-            dma((len(members),)), dma((len(members),)),
+            dma((len(members), ny // LANES)), dma((len(members), ny // LANES)),
         ],
         compiler_params=pltpu.CompilerParams(
             collective_id=0, has_side_effects=True, vmem_limit_bytes=40 * 2**20),

time: 29 us -> 27.8 us (0.959)
  Pallas kernels: 28.3 us -> 27 us
    pallas_call x1, Pallas kernels: 26.6 us -> 25.4 us  [per_device(): pl.pallas_call(functools.partial(kernel, gxn, gzn, cells), out_shape=(hel...]
where the time goes in v2:
time: 27.8 us; the launch traced here: 27.6 us
  Pallas kernels  27 us (97%)
  between operations  0.64 us (2%)
    pallas_call x1, Pallas kernels, per_device(): pl.pallas_call(functools.partial(kernel, gxn, gzn, cells), out_shape=(hel...  25.4 us
    pallas_call x1, Pallas kernels, per_device(): pl.pallas_call(finish, out_shape=(field, field, field, jax.ShapeDtypeStru...  1.61 us

profile of v2, /device:TPU:0, one launch (start us, length us, event | category | flops | bytes accessed | tf_op | source)
XLA Modules:
  0.0 27.6 jit_solution(1941453132786628424)
XLA Ops:
  0.6 25.4 %shard_map.57 = (f32[8,32,384]{2,1,0:T(8,128)S(1)}, f32[8,32,384]{2,1,0:T(8,128)S(1)}, f32[8,32,384]{2,1,0:T(8,128)S(1)}, f32[2,384]{1,0:T(2,128)S(1)}) custom-call(f32[1,385]{1,0:T(1,128)} %bitcast.1, f32[3,8,32,384]{3,2,1,0:T(8,128)} %vel_ref.1), custom_call_target="tpu_custom_call" | custom-call | tf_op jit(solution)/shard_map/pallas_call | solution.py:391
  26.0 1.6 %shard_map.58 = (f32[8,32,384]{2,1,0:T(8,128)}, f32[8,32,384]{2,1,0:T(8,128)}, f32[8,32,384]{2,1,0:T(8,128)}, f32[384]{0:T(512)}) custom-call(f32[8,32,384]{2,1,0:T(8,128)S(1)} %get-tuple-element.8.size_ref, f32[8,32,384]{2,1,0:T(8,128)S(1)} %get-tuple-element.9.lm_ref, f32[8,32,384]{2,1,0:T(8,128)S(1)} %get-tuple-element.10.mm_ref, ...), custom_call_target="tpu_custom_call" | custom-call | tf_op jit(solution)/shard_map/pallas_call | solution.py:416

commit v3 on v2

--- a/solution.py
+++ b/solution.py
@@ -19,19 +19,19 @@
     return jnp.exp(jnp.log(0.5 * span) * (2.0 / 3.0))
 
 
-def finish(size_ref, lm_ref, mm_ref, coef_ref, eddy_out, lm_out, mm_out, coef_out, eddy_s, sem):
-    nx, _, ny = size_ref.shape
+def finish(size_ref, lm_ref, mm_ref, coef_ref, eddy_out, lm_out, mm_out, coef_out, eddy_s, coef_s, sem):
+    nx = size_ref.shape[0]
     copies = [pltpu.make_async_copy(lm_ref, lm_out, sem.at[0]), pltpu.make_async_copy(mm_ref, mm_out, sem.at[1])]
+    coef_s[...] = coef_ref[0:1].reshape(coef_s.shape)
+    copies.append(pltpu.make_async_copy(coef_s, coef_out, sem.at[2]))
     for copy in copies:
         copy.start()
     factor = coef_ref[1:2]
     for r in range(0, nx, 2):
         rows = pl.ds(r, 2)
         eddy_s[rows] = factor * size_ref[rows]
-        copy = pltpu.make_async_copy(eddy_s.at[rows], eddy_out.at[rows], sem.at[2 + r // 2])
-        copy.start()
-        copies.append(copy)
-    coef_out[...] = coef_ref[0:1].reshape(ny)
+        pltpu.make_async_copy(eddy_s.at[rows], eddy_out.at[rows], sem.at[3]).start()
+    copies.append(pltpu.make_async_copy(eddy_s, eddy_out, sem.at[3]))
     for copy in copies:
         copy.wait()
 
@@ -72,7 +72,7 @@
         signal(barrier, device)
     loads = []
     for n, (lo, hi) in enumerate(((0, 2), (nx - 2, nx), (2, nx - 2))):
-        loads.append(pltpu.make_async_copy(vel_ref.at[:, lo:hi], pad.at[:, lo + 2:hi + 2, 0:nz], load_sem.at[n]))
+        loads.append(pltpu.make_async_copy(vel_ref.at[:, lo:hi], pad.at[:, lo + 2:hi + 2, 0:nz], load_sem.at[n // 2]))
     for load in loads:
         load.start()
     gap_load = pltpu.make_async_copy(gap_hbm, gap_ref, gap_sem)
@@ -90,50 +90,45 @@
     order = (parity, 1 - parity)
     sides = [side_rows(side) for side in order]
 
+    def group_of(n):
+        return 0 if n in EDGES else 1 if n in NEAR else 2 + (n - 5) // 3
+
     def x_pieces(p):
         side, rows = order[p], sides[p]
         device = (lax.select(side == 0, along_x(-1)[0], along_x(1)[0]), gz)
-        there = 1 - side
         plan = []
-        both = (2, rows["both_from"], rows["both_to"], rows["both"])
-        near = (1, rows["near_from"], rows["to_halo"], rows["halo"])
-        far = (1, rows["far_from"], rows["to_far"], rows["far"])
+        both = (2, rows["both_from"], rows["both_to"])
+        near = (1, rows["near_from"], rows["to_halo"])
+        far = (1, rows["far_from"], rows["to_far"])
         for ks in (pl.ds(0, 2), pl.ds(nz - 2, 2)):
-            plan.append((both, ks, pl.ds(0, ny)))
+            plan.append((*both, ks, pl.ds(0, ny)))
         inner = (pl.ds(2, 6), pl.ds(8, nz - 16), pl.ds(nz - 8, 6))
         for ks in inner:
-            plan.append((near, ks, pl.ds(0, ny)))
+            plan.append((*near, ks, pl.ds(0, ny)))
         for cols in tiles:
             for ks in inner:
-                plan.append((far, ks, cols))
-        out = []
-        for n, ((deep, src, dst, here), ks, cols) in enumerate(plan):
-            give = remote(pad.at[:, pl.ds(src, deep), ks, cols], pad.at[:, pl.ds(dst, deep), ks, cols],
-                          xs_sem.at[n, side], xr_sem.at[n, there], device)
-            got = pad.at[:, pl.ds(here, deep), ks, cols]
-            got = remote(got, got, xs_sem.at[n, side], xr_sem.at[n, side], device)
-            out.append((give, got))
-        return out
+                plan.append((*far, ks, cols))
+        return [remote(pad.at[:, pl.ds(src, deep), ks, cols], pad.at[:, pl.ds(dst, deep), ks, cols],
+                       xs_sem, xr_sem.at[group_of(n)], device)
+                for n, (deep, src, dst, ks, cols) in enumerate(plan)]
 
     pieces = [x_pieces(p) for p in range(2)]
-    k_up = remote(pad.at[:, 2:nx + 2, nz - 2:nz], pad.at[:, 2:nx + 2, wide - 2:wide], ks_sem.at[0], kr_sem.at[0], along_z(1))
-    k_down = remote(pad.at[:, 2:nx + 2, 0:2], pad.at[:, 2:nx + 2, nz:nz + 2], ks_sem.at[1], kr_sem.at[1], along_z(-1))
+    k_up = remote(pad.at[:, 2:nx + 2, nz - 2:nz], pad.at[:, 2:nx + 2, wide - 2:wide], ks_sem, kr_sem, along_z(1))
+    k_down = remote(pad.at[:, 2:nx + 2, 0:2], pad.at[:, 2:nx + 2, nz:nz + 2], ks_sem, kr_sem, along_z(-1))
 
     def far(t):
         return tuple(range(5 + 3 * t, 8 + 3 * t))
+
+    def wait_for(columns, sem, cols=pl.ds(0, ny)):
+        ref = pad.at[:, 0:columns // 8, 0:8, cols]
+        remote(ref, ref, sem, sem, (gx, gz)).wait_recv()
 
     def send(*which):
         for n in which:
             for p in range(2):
-                pieces[p][n][0].start()
-
-    def take(*which):
-        for n in which:
-            for p in range(2):
-                pieces[p][n][1].wait_recv()
-
-    for load in loads[:2]:
-        load.wait()
+                pieces[p][n].start()
+
+    pltpu.make_async_copy(vel_ref.at[:, 0:4], pad.at[:, 0:4, 0:nz], load_sem.at[0]).wait()
     pl.semaphore_wait(barrier, 4)
     send(*EDGES, *NEAR)
     loads[2].wait()
@@ -282,33 +277,31 @@
             return carry
         lax.fori_loop(lo, hi, step, 0)
 
-    k_up.wait_recv()
-    k_down.wait_recv()
+    wait_for(4 * nx, kr_sem)
     over(3, nx + 1, first)
     learn()
-    take(*EDGES)
+    smooth_row(2)
+    smooth_row(nx + 1)
+    over(4, nx, second)
+    send(*far(0))
+    send(*far(1))
+    wait_for(16, xr_sem.at[0])
     relayed = []
     for p in range(2):
         rows = pl.ds(sides[p]["both"], 2)
         for n, (src, dst, device) in enumerate(((nz - 2, wide - 2, along_z(1)), (0, nz, along_z(-1)))):
-            relayed.append(remote(pad.at[:, rows, pl.ds(src, 2)], pad.at[:, rows, pl.ds(dst, 2)], cs_sem.at[n, order[p]], cr_sem.at[n, order[p]], device))
+            relayed.append(remote(pad.at[:, rows, pl.ds(src, 2)], pad.at[:, rows, pl.ds(dst, 2)], cs_sem, cr_sem, device))
     for copy in relayed:
         copy.start()
-    send(*far(0))
-    smooth_row(2)
-    smooth_row(nx + 1)
-    over(4, nx, second)
-    send(*far(1))
 
     def both(body):
         for p in range(2):
             body(p, sides[p])
 
-    take(*NEAR)
+    wait_for(2 * (nz - 4), xr_sem.at[1])
     send(*far(2))
     learn()
-    for copy in relayed:
-        copy.wait_recv()
+    wait_for(16, cr_sem)
 
     def ready(p, rows):
         first(rows["edge"])
@@ -338,14 +331,14 @@
         acc = accs[n].at[t]
         acc[slot] = value
         for device in devices:
-            remote(acc.at[slot], acc.at[slot], as_sem.at[n, t], ar_sem.at[n, t], device).start()
+            remote(acc.at[slot], acc.at[slot], as_sem.at[n], ar_sem.at[n, t], device).start()
 
     def gathered(n, t):
         acc, count = accs[n].at[t], len(rounds[n][1])
-        return remote(acc.at[0:count], acc.at[0:count], as_sem.at[n, t], ar_sem.at[n, t], (gx, gz))
+        return remote(acc.at[0:count], acc.at[0:count], as_sem.at[n], ar_sem.at[n, t], (gx, gz))
 
     for t, cols in enumerate(tiles):
-        take(*far(t))
+        wait_for(2 * (nz - 4), xr_sem.at[2 + t], tiles[0])
 
         def finish_rows(p, rows):
             stress_tile(rows["halo"], cols, False, p)
@@ -364,14 +357,13 @@
                 coefficient = total[0:1] / cells / (total[1:2] / cells + 1e-06)
                 out_coef_ref[0:1, cols] = coefficient
                 out_coef_ref[1:2, cols] = coefficient * coef_ref[4:5, cols]
-    sent = [gathered(n, t) for n in range(len(rounds)) for t in range(len(tiles))]
-    k_up.wait_send()
-    k_down.wait_send()
-    for p in range(2):
-        for copy, _ in pieces[p]:
-            copy.wait_send()
-    for copy in relayed + sent:
-        copy.wait_send()
+    wait_for(4 * nx, ks_sem)
+    block = pad.at[:, 0:4, 0:nz]
+    remote(block, block, xs_sem, xs_sem, (gx, gz)).wait_send()
+    wait_for(16, cs_sem)
+    for n, (_, devices) in enumerate(rounds):
+        acc = accs[n].at[:, 0:len(devices)]
+        remote(acc, acc, as_sem.at[n], as_sem.at[n], (gx, gz)).wait_send()
 
 
 def per_device(velocity, y_gap):
@@ -383,7 +375,6 @@
     wide = nz + RIM
     dma, flag = pltpu.SemaphoreType.DMA, pltpu.SemaphoreType.REGULAR
     members = (gxn * gzn,) if gxn * gzn <= DIRECT else (gzn, gxn)
-    parts = 5 + 3 * (ny // LANES)
     gaps = y_gap.reshape(1, ny + 1)
     near = pl.BlockSpec(memory_space=pltpu.VMEM)
     far = pl.BlockSpec(memory_space=pl.ANY)
@@ -406,9 +397,9 @@
             pltpu.VMEM((2, 8, ny), f32),
             tuple(pltpu.VMEM((ny // LANES, n, 2, LANES), f32) for n in members),
             pltpu.VMEM((1, ny + 1), f32), dma,
-            dma((3,)), dma((parts, 2)), dma((parts, 2)), dma((2,)), dma((2,)), dma((2, 2)), dma((2, 2)),
+            dma((2,)), dma, dma((2 + ny // LANES,)), dma, dma, dma, dma,
             flag((max(len(doublings(gxn)), 1),)), flag((max(len(doublings(gzn)), 1),)), flag,
-            dma((len(members), ny // LANES)), dma((len(members), ny // LANES)),
+            dma((len(members),)), dma((len(members), ny // LANES)),
         ],
         compiler_params=pltpu.CompilerParams(
             collective_id=0, has_side_effects=True, vmem_limit_bytes=40 * 2**20),
@@ -417,8 +408,8 @@
         finish,
         out_shape=(field, field, field, jax.ShapeDtypeStruct((ny,), f32)),
         in_specs=[near] * 4,
-        out_specs=(far, far, far, near),
-        scratch_shapes=[pltpu.VMEM((nx, nz, ny), f32), dma((2 + (nx + 1) // 2,))],
+        out_specs=(far,) * 4,
+        scratch_shapes=[pltpu.VMEM((nx, nz, ny), f32), pltpu.VMEM((ny,), f32), dma((4,))],
         compiler_params=pltpu.CompilerParams(vmem_limit_bytes=8 * 2**20),
     )(size, lm, mm, coefficient)
 

time: 27.8 us -> 26.5 us (0.953)
  Pallas kernels: 27 us -> 25.7 us
    pallas_call x1, Pallas kernels: 25.4 us -> 24.7 us  [per_device(): pl.pallas_call(functools.partial(kernel, gxn, gzn, cells), out_shape=(hel...]
    pallas_call x1, Pallas kernels: 1.61 us -> 1.04 us  [per_device(): pl.pallas_call(finish, out_shape=(field, field, field, jax.ShapeDtypeStru...]
where the time goes in v3:
time: 26.5 us; the launch traced here: 26.4 us
  Pallas kernels  25.7 us (97%)
  between operations  0.64 us (2%)
    pallas_call x1, Pallas kernels, per_device(): pl.pallas_call(functools.partial(kernel, gxn, gzn, cells), out_shape=(hel...  24.7 us
    pallas_call x1, Pallas kernels, per_device(): pl.pallas_call(finish, out_shape=(field, field, field, jax.ShapeDtypeStru...  1.04 us

profile of v3, /device:TPU:0, one launch (start us, length us, event | category | flops | bytes accessed | tf_op | source)
XLA Modules:
  0.0 26.4 jit_solution(8568719591194221891)
XLA Ops:
  0.6 24.7 %shard_map.57 = (f32[8,32,384]{2,1,0:T(8,128)S(1)}, f32[8,32,384]{2,1,0:T(8,128)S(1)}, f32[8,32,384]{2,1,0:T(8,128)S(1)}, f32[2,384]{1,0:T(2,128)S(1)}) custom-call(f32[1,385]{1,0:T(1,128)} %bitcast.1, f32[3,8,32,384]{3,2,1,0:T(8,128)} %vel_ref.1), custom_call_target="tpu_custom_call" | custom-call | tf_op jit(solution)/shard_map/pallas_call | solution.py:382
  25.3 1.0 %shard_map.58 = (f32[8,32,384]{2,1,0:T(8,128)}, f32[8,32,384]{2,1,0:T(8,128)}, f32[8,32,384]{2,1,0:T(8,128)}, f32[384]{0:T(512)}) custom-call(f32[8,32,384]{2,1,0:T(8,128)S(1)} %get-tuple-element.8.size_ref, f32[8,32,384]{2,1,0:T(8,128)S(1)} %get-tuple-element.9.lm_ref, f32[8,32,384]{2,1,0:T(8,128)S(1)} %get-tuple-element.10.mm_ref, ...), custom_call_target="tpu_custom_call" | custom-call | tf_op jit(solution)/shard_map/pallas_call | solution.py:407

commit v4 on v3

--- a/solution.py
+++ b/solution.py
@@ -320,21 +320,21 @@
         pass
     here = gx * gzn + gz
     if direct:
-        rounds = [(here, [(lax.rem(gx + dx, gxn), lax.rem(gz + dz, gzn))
-                          for dx in sorted(range(gxn), key=lambda d: -min(d, gxn - d))
-                          for dz in range(gzn) if dx or dz])]
+        rounds = [(here, [(ox, oz) for ox in range(gxn) for oz in range(gzn)], gxn * gzn - 1)]
     else:
-        rounds = [(gz, [along_z(d) for d in range(1, gzn)]), (gx, [along_x(d) for d in range(1, gxn)])]
+        rounds = [(gz, [(gx, oz) for oz in range(gzn)], gzn - 1), (gx, [(ox, gz) for ox in range(gxn)], gxn - 1)]
 
     def spread(n, t, value):
-        slot, devices = rounds[n]
+        slot, devices, _ = rounds[n]
         acc = accs[n].at[t]
         acc[slot] = value
         for device in devices:
-            remote(acc.at[slot], acc.at[slot], as_sem.at[n], ar_sem.at[n, t], device).start()
+            @pl.when((device[0] != gx) | (device[1] != gz))
+            def _():
+                remote(acc.at[slot], acc.at[slot], as_sem.at[n], ar_sem.at[n, t], device).start()
 
     def gathered(n, t):
-        acc, count = accs[n].at[t], len(rounds[n][1])
+        acc, count = accs[n].at[t], rounds[n][2]
         return remote(acc.at[0:count], acc.at[0:count], as_sem.at[n], ar_sem.at[n, t], (gx, gz))
 
     for t, cols in enumerate(tiles):
@@ -361,8 +361,8 @@
     block = pad.at[:, 0:4, 0:nz]
     remote(block, block, xs_sem, xs_sem, (gx, gz)).wait_send()
     wait_for(16, cs_sem)
-    for n, (_, devices) in enumerate(rounds):
-        acc = accs[n].at[:, 0:len(devices)]
+    for n, (_, _, count) in enumerate(rounds):
+        acc = accs[n].at[:, 0:count]
         remote(acc, acc, as_sem.at[n], as_sem.at[n], (gx, gz)).wait_send()
 
 

time: 26.5 us -> 26.3 us (level)
  no operation moved by 1% of the time
where the time goes in v4:
time: 26.3 us; the launch traced here: 26.1 us
  Pallas kernels  25.5 us (97%)
  between operations  0.64 us (2%)
    pallas_call x1, Pallas kernels, per_device(): pl.pallas_call(functools.partial(kernel, gxn, gzn, cells), out_shape=(hel...  24.4 us
    pallas_call x1, Pallas kernels, per_device(): pl.pallas_call(finish, out_shape=(field, field, field, jax.ShapeDtypeStru...  1.04 us

profile of v4, /device:TPU:0, one launch (start us, length us, event | category | flops | bytes accessed | tf_op | source)
XLA Modules:
  0.0 26.1 jit_solution(1621379643658193358)
XLA Ops:
  0.6 24.4 %shard_map.57 = (f32[8,32,384]{2,1,0:T(8,128)S(1)}, f32[8,32,384]{2,1,0:T(8,128)S(1)}, f32[8,32,384]{2,1,0:T(8,128)S(1)}, f32[2,384]{1,0:T(2,128)S(1)}) custom-call(f32[1,385]{1,0:T(1,128)} %bitcast.1, f32[3,8,32,384]{3,2,1,0:T(8,128)} %vel_ref.1), custom_call_target="tpu_custom_call" | custom-call | tf_op jit(solution)/shard_map/pallas_call | solution.py:382
  25.1 1.0 %shard_map.58 = (f32[8,32,384]{2,1,0:T(8,128)}, f32[8,32,384]{2,1,0:T(8,128)}, f32[8,32,384]{2,1,0:T(8,128)}, f32[384]{0:T(512)}) custom-call(f32[8,32,384]{2,1,0:T(8,128)S(1)} %get-tuple-element.8.size_ref, f32[8,32,384]{2,1,0:T(8,128)S(1)} %get-tuple-element.9.lm_ref, f32[8,32,384]{2,1,0:T(8,128)S(1)} %get-tuple-element.10.mm_ref, ...), custom_call_target="tpu_custom_call" | custom-call | tf_op jit(solution)/shard_map/pallas_call | solution.py:407

commit v5 on v4

--- a/solution.py
+++ b/solution.py
@@ -45,7 +45,7 @@
 
 
 def kernel(gxn, gzn, cells, gap_hbm, vel_ref, size_s, lm_s, mm_s, out_coef_ref,
-           pad, zvel, zpair, zstress, slope, tslope, vslope, leon_ref, coef_ref, sums, accs,
+           pad, zvel, zpair, zstress, slope, tslope, vslope, strain_ref, test_ref, rest_ref, leon_ref, coef_ref, sums, accs,
            gap_ref, gap_sem, load_sem, xs_sem, xr_sem, ks_sem, kr_sem, cs_sem, cr_sem,
            near_x, near_z, near_all, as_sem, ar_sem):
     gx, gz = lax.axis_index("gx"), lax.axis_index("gz")
@@ -82,13 +82,14 @@
         def pick(low, high):
             return lax.select(side == 0, low, high)
         return dict(
-            inner=pick(3, nx), edge=pick(2, nx + 1), halo=pick(1, nx + 2), far=pick(0, nx + 3),
+            other=pick(4, nx - 1), inner=pick(3, nx), edge=pick(2, nx + 1), halo=pick(1, nx + 2), far=pick(0, nx + 3),
             to_halo=pick(nx + 2, 1), to_far=pick(nx + 3, 0), near_from=pick(2, nx + 1), far_from=pick(3, nx),
             both_from=pick(2, nx), both_to=pick(nx + 2, 0), both=pick(0, nx + 2))
 
     parity = lax.rem(gx, 2)
     order = (parity, 1 - parity)
     sides = [side_rows(side) for side in order]
+    signs = [lax.select(side == 0, 1.0, -1.0) for side in order]
 
     def group_of(n):
         return 0 if n in EDGES else 1 if n in NEAR else 2 + (n - 5) // 3
@@ -191,25 +192,26 @@
         for cols in tiles:
             smooth_tile(r, cols)
 
-    def first_slope(r, n=2):
+    def first_slope(r):
         for c in range(3):
-            slope[n, c] = lane_slope(pad[c, r])
-
-    def stress_tile(r, cols, inside, side=2):
+            slope[c] = lane_slope(pad[c, r])
+
+    def strain_size(f):
+        square = [s * s for s in f]
+        return jnp.sqrt(0.5 * (square[0] + square[1] + square[2]) + 0.25 * (square[3] + square[4] + square[5]))
+
+    def stress_tile(r, cols):
         u = [pad[c, r, :, cols] for c in range(3)]
         a = [pad[c, r + 1, :, cols] - pad[c, r - 1, :, cols] for c in range(3)]
         b = []
         for c in range(3):
             prev, nxt = pltpu.roll(u[c], 1, 0), pltpu.roll(u[c], wide - 1, 0)
             b.append(nxt - prev)
-            if inside:
-                zvel[c, r, :, cols] = (nxt + prev) + 2.0 * u[c]
-        d = [slope[side, c, :, cols] for c in range(3)]
+            zvel[c, r, :, cols] = (nxt + prev) + 2.0 * u[c]
+        d = [slope[c, :, cols] for c in range(3)]
         strain = [a[0], d[1], b[2], d[0] + a[1], b[0] + a[2], b[1] + d[2]]
-        square = [s * s for s in strain]
-        size = jnp.sqrt(0.5 * (square[0] + square[1] + square[2]) + 0.25 * (square[3] + square[4] + square[5]))
-        if inside:
-            size_s[r - 2, :, cols] = size[:nz]
+        size = strain_size(strain)
+        size_s[r - 2, :, cols] = size[:nz]
         for n in range(6):
             zstress[n, r, :, cols] = filtered(size * strain[n])[:nz]
 
@@ -221,39 +223,30 @@
     def first(r):
         first_slope(r)
         for cols in tiles:
-            stress_tile(r, cols, True)
+            stress_tile(r, cols)
             pair_tile(r, cols)
 
-    def second_slope(r, n=2):
+    def second_slope(r):
         for c in range(3):
             v = (zvel[c, r - 1] + zvel[c, r + 1]) + 2.0 * zvel[c, r]
-            tslope[n, c] = v
-            vslope[n, c] = lane_slope(v)
-
-    def leonard(r, cols, side=2):
-        v = [tslope[side, c, 0:nz, cols] for c in range(3)]
+            tslope[c] = v
+            vslope[c] = lane_slope(v)
+
+    def leonard(r, cols):
+        v = [tslope[c, 0:nz, cols] for c in range(3)]
         out = []
         for n, (i, j) in enumerate(PAIRS):
             pair = (zpair[n, r - 1, :, cols] + zpair[n, r + 1, :, cols]) + 2.0 * zpair[n, r, :, cols]
             out.append(pair - v[i] * v[j] * 0.0625)
         return out
 
-    def second_tile(r, cols, side=2, leon=None):
+    def contract(r, cols, test, stress, leon):
         w = coef_ref[2:3, cols]
         w2 = coef_ref[3:4, cols]
-        v_wide = [tslope[side, c, :, cols] for c in range(3)]
-        a = [(zvel[c, r + 2, 0:nz, cols] - zvel[c, r - 2, 0:nz, cols])
-             + 2.0 * (zvel[c, r + 1, 0:nz, cols] - zvel[c, r - 1, 0:nz, cols]) for c in range(3)]
-        b = [(pltpu.roll(f, wide - 1, 0) - pltpu.roll(f, 1, 0))[:nz] for f in v_wide]
-        d = [vslope[side, c, 0:nz, cols] for c in range(3)]
-        test = [a[0], d[1], b[2], d[0] + a[1], b[0] + a[2], b[1] + d[2]]
-        square = [s * s for s in test]
-        q = 0.25 * jnp.sqrt(0.5 * (square[0] + square[1] + square[2]) + 0.25 * (square[3] + square[4] + square[5]))
+        q = 0.25 * strain_size(test)
         lm, mm_diag, mm_off = 0.0, 0.0, 0.0
-        leon = leon or leonard(r, cols, side)
         for n in range(6):
-            stress = (zstress[n, r - 1, :, cols] + zstress[n, r + 1, :, cols]) + 2.0 * zstress[n, r, :, cols]
-            model = stress - q * test[n]
+            model = stress[n] - q * test[n]
             lm = lm + leon[n] * model
             if n < 3:
                 mm_diag = mm_diag + model * model
@@ -265,6 +258,16 @@
         mm_s[r - 2, :, cols] = mm
         for n, f in enumerate((lm, mm)):
             sums[n, :, cols] += jnp.sum(f.reshape(nz // 8, 8, LANES), axis=0)
+
+    def second_tile(r, cols):
+        v_wide = [tslope[c, :, cols] for c in range(3)]
+        a = [(zvel[c, r + 2, 0:nz, cols] - zvel[c, r - 2, 0:nz, cols])
+             + 2.0 * (zvel[c, r + 1, 0:nz, cols] - zvel[c, r - 1, 0:nz, cols]) for c in range(3)]
+        b = [(pltpu.roll(f, wide - 1, 0) - pltpu.roll(f, 1, 0))[:nz] for f in v_wide]
+        d = [vslope[c, 0:nz, cols] for c in range(3)]
+        test = [a[0], d[1], b[2], d[0] + a[1], b[0] + a[2], b[1] + d[2]]
+        stress = [(zstress[n, r - 1, :, cols] + zstress[n, r + 1, :, cols]) + 2.0 * zstress[n, r, :, cols] for n in range(6)]
+        contract(r, cols, test, stress, leonard(r, cols))
 
     def second(r):
         second_slope(r)
@@ -304,15 +307,29 @@
     wait_for(16, cr_sem)
 
     def ready(p, rows):
-        first(rows["edge"])
-        smooth_row(rows["halo"])
+        halo, edge = rows["halo"], rows["edge"]
+        first(edge)
+        smooth_row(halo)
         second(rows["inner"])
-        first_slope(rows["halo"], p)
-        second_slope(rows["edge"], p)
+        first_slope(halo)
+        second_slope(edge)
         for cols in tiles:
-            pair_tile(rows["halo"], cols)
-            for n, f in enumerate(leonard(rows["edge"], cols, p)):
-                leon_ref[p, n, :, cols] = f
+            pair_tile(halo, cols)
+            u = [pad[c, halo, :, cols] for c in range(3)]
+            b = [pltpu.roll(f, wide - 1, 0) - pltpu.roll(f, 1, 0) for f in u]
+            d = [slope[c, :, cols] for c in range(3)]
+            for n, f in enumerate((d[1], b[2], d[0], b[0], b[1] + d[2])):
+                strain_ref[p, n, :, cols] = f
+            v = [tslope[c, :, cols] for c in range(3)]
+            b = [(pltpu.roll(f, wide - 1, 0) - pltpu.roll(f, 1, 0))[:nz] for f in v]
+            a = [signs[p] * zvel[c, rows["other"], 0:nz, cols] + 2.0 * (zvel[c, edge + 1, 0:nz, cols] - zvel[c, edge - 1, 0:nz, cols])
+                 for c in range(3)]
+            d = [vslope[c, 0:nz, cols] for c in range(3)]
+            leon = leonard(edge, cols)
+            for n, f in enumerate((a[0], d[1], b[2], d[0] + a[1], b[0] + a[2], b[1] + d[2])):
+                test_ref[p, n, :, cols] = f
+                leon_ref[p, n, :, cols] = leon[n]
+                rest_ref[p, n, :, cols] = zstress[n, rows["inner"], :, cols] + 2.0 * zstress[n, edge, :, cols]
 
     ready(0, sides[0])
     ready(1, sides[1])
@@ -341,9 +358,16 @@
         wait_for(2 * (nz - 4), xr_sem.at[2 + t], tiles[0])
 
         def finish_rows(p, rows):
-            stress_tile(rows["halo"], cols, False, p)
-            smooth_tile(rows["far"], cols)
-            second_tile(rows["edge"], cols, p, [leon_ref[p, n, :, cols] for n in range(6)])
+            u = [pad[c, rows["far"], :, cols] for c in range(3)]
+            a = [signs[p] * (pad[c, rows["edge"], :, cols] - u[c]) for c in range(3)]
+            part = [strain_ref[p, n, :, cols] for n in range(5)]
+            strain = [a[0], part[0], part[1], part[2] + a[1], part[3] + a[2], part[4]]
+            size = strain_size(strain)
+            part = [test_ref[p, n, :, cols] for n in range(6)]
+            a = [signs[p] * filtered(f)[:nz] for f in u]
+            test = [part[0] - a[0], part[1], part[2], part[3] - a[1], part[4] - a[2], part[5]]
+            stress = [rest_ref[p, n, :, cols] + filtered(size * strain[n])[:nz] for n in range(6)]
+            contract(rows["edge"], cols, test, stress, [leon_ref[p, n, :, cols] for n in range(6)])
 
         both(finish_rows)
         spread(0, t, jnp.sum(sums[:, :, cols], axis=1))
@@ -389,9 +413,12 @@
             pltpu.VMEM((3, nx + 4, wide, ny), f32),
             pltpu.VMEM((6, nx + 4, nz, ny), f32),
             pltpu.VMEM((6, nx + 4, nz, ny), f32),
-            pltpu.VMEM((3, 3, wide, ny), f32),
-            pltpu.VMEM((3, 3, wide, ny), f32),
-            pltpu.VMEM((3, 3, wide, ny), f32),
+            pltpu.VMEM((3, wide, ny), f32),
+            pltpu.VMEM((3, wide, ny), f32),
+            pltpu.VMEM((3, wide, ny), f32),
+            pltpu.VMEM((2, 5, wide, ny), f32),
+            pltpu.VMEM((2, 6, nz, ny), f32),
+            pltpu.VMEM((2, 6, nz, ny), f32),
             pltpu.VMEM((2, 6, nz, ny), f32),
             pltpu.VMEM((8, ny), f32),
             pltpu.VMEM((2, 8, ny), f32),

time: 26.3 us -> 26.2 us (level)
  no operation moved by 1% of the time
where the time goes in v5:
time: 26.2 us; the launch traced here: 26 us
  Pallas kernels  25.4 us (97%)
  between operations  0.64 us (2%)
    pallas_call x1, Pallas kernels, per_device(): pl.pallas_call(functools.partial(kernel, gxn, gzn, cells), out_shape=(hel...  24.4 us
    pallas_call x1, Pallas kernels, per_device(): pl.pallas_call(finish, out_shape=(field, field, field, jax.ShapeDtypeStru...  1.04 us

profile of v5, /device:TPU:0, one launch (start us, length us, event | category | flops | bytes accessed | tf_op | source)
XLA Modules:
  0.0 26.0 jit_solution(13648083638694544890)
XLA Ops:
  0.6 24.4 %shard_map.57 = (f32[8,32,384]{2,1,0:T(8,128)S(1)}, f32[8,32,384]{2,1,0:T(8,128)S(1)}, f32[8,32,384]{2,1,0:T(8,128)S(1)}, f32[2,384]{1,0:T(2,128)S(1)}) custom-call(f32[1,385]{1,0:T(1,128)} %bitcast.1, f32[3,8,32,384]{3,2,1,0:T(8,128)} %vel_ref.1), custom_call_target="tpu_custom_call" | custom-call | tf_op jit(solution)/shard_map/pallas_call | solution.py:406
  25.0 1.0 %shard_map.58 = (f32[8,32,384]{2,1,0:T(8,128)}, f32[8,32,384]{2,1,0:T(8,128)}, f32[8,32,384]{2,1,0:T(8,128)}, f32[384]{0:T(512)}) custom-call(f32[8,32,384]{2,1,0:T(8,128)S(1)} %get-tuple-element.8.size_ref, f32[8,32,384]{2,1,0:T(8,128)S(1)} %get-tuple-element.9.lm_ref, f32[8,32,384]{2,1,0:T(8,128)S(1)} %get-tuple-element.10.mm_ref, ...), custom_call_target="tpu_custom_call" | custom-call | tf_op jit(solution)/shard_map/pallas_call | solution.py:434

commit v6 on v5

--- a/solution.py
+++ b/solution.py
@@ -45,9 +45,9 @@
 
 
 def kernel(gxn, gzn, cells, gap_hbm, vel_ref, size_s, lm_s, mm_s, out_coef_ref,
-           pad, zvel, zpair, zstress, slope, tslope, vslope, strain_ref, test_ref, rest_ref, leon_ref, coef_ref, sums, accs,
+           pad, zvel, zpair, zstress, slope, tslope, vslope, strain_ref, test_ref, rest_ref, leon_ref, coef_ref, sums, accs, via_ref, count_ref,
            gap_ref, gap_sem, load_sem, xs_sem, xr_sem, ks_sem, kr_sem, cs_sem, cr_sem,
-           near_x, near_z, near_all, as_sem, ar_sem):
+           near_x, near_z, near_all, wrap_sem, via_sem, as_sem, ar_sem):
     gx, gz = lax.axis_index("gx"), lax.axis_index("gz")
     nx, nz, ny = vel_ref.shape[1:]
     wide = nz + RIM
@@ -68,8 +68,14 @@
             device_id=device, device_id_type=MESH)
 
     barrier = pltpu.get_barrier_semaphore()
-    for device in (along_x(1), along_x(-1), along_z(1), along_z(-1)):
+    for device in (along_x(-1), along_z(1), along_z(-1)):
         signal(barrier, device)
+    ahead, behind = gx < gxn - 1, gx > 0
+
+    @pl.when(ahead)
+    def _():
+        signal(barrier, along_x(1))
+
     loads = []
     for n, (lo, hi) in enumerate(((0, 2), (nx - 2, nx), (2, nx - 2))):
         loads.append(pltpu.make_async_copy(vel_ref.at[:, lo:hi], pad.at[:, lo + 2:hi + 2, 0:nz], load_sem.at[n // 2]))
@@ -93,6 +99,8 @@
 
     def group_of(n):
         return 0 if n in EDGES else 1 if n in NEAR else 2 + (n - 5) // 3
+
+    inner = (pl.ds(2, 6), pl.ds(8, nz - 16), pl.ds(nz - 8, 6))
 
     def x_pieces(p):
         side, rows = order[p], sides[p]
@@ -103,7 +111,6 @@
         far = (1, rows["far_from"], rows["to_far"])
         for ks in (pl.ds(0, 2), pl.ds(nz - 2, 2)):
             plan.append((*both, ks, pl.ds(0, ny)))
-        inner = (pl.ds(2, 6), pl.ds(8, nz - 16), pl.ds(nz - 8, 6))
         for ks in inner:
             plan.append((*near, ks, pl.ds(0, ny)))
         for cols in tiles:
@@ -114,6 +121,16 @@
                 for n, (deep, src, dst, ks, cols) in enumerate(plan)]
 
     pieces = [x_pieces(p) for p in range(2)]
+    detour = gxn >= 4 and gxn % 2 == 0
+    odd = parity == 1
+    sends_via = (odd & (gx < gxn - 1)) | (gx == 0)
+    carries = (jnp.logical_not(odd) & (gx < gxn - 2)) | (gx == 1)
+    partner = lax.select(odd, along_x(-1)[0], along_x(1)[0])
+    beyond = lax.select(odd, along_x(-2)[0], along_x(2)[0])
+    via = [remote(pad.at[:, pl.ds(sides[0]["far_from"], 1), ks, tiles[-1]], via_ref.at[:, :, ks],
+                  xs_sem, via_sem.at[0], (partner, gz)) for ks in inner]
+    onward = [remote(via_ref.at[:, :, ks], pad.at[:, pl.ds(lax.select(odd, nx + 3, 0), 1), ks, tiles[-1]],
+                     via_sem.at[1], xr_sem.at[1 + len(tiles)], (beyond, gz)) for ks in inner]
     k_up = remote(pad.at[:, 2:nx + 2, nz - 2:nz], pad.at[:, 2:nx + 2, wide - 2:wide], ks_sem, kr_sem, along_z(1))
     k_down = remote(pad.at[:, 2:nx + 2, 0:2], pad.at[:, 2:nx + 2, nz:nz + 2], ks_sem, kr_sem, along_z(-1))
 
@@ -124,14 +141,42 @@
         ref = pad.at[:, 0:columns // 8, 0:8, cols]
         remote(ref, ref, sem, sem, (gx, gz)).wait_recv()
 
-    def send(*which):
+    def send(*which, sides=(0, 1)):
         for n in which:
-            for p in range(2):
-                pieces[p][n].start()
+            for p in sides:
+                if detour and p == 0 and n in far(len(tiles) - 1):
+                    pl.when(jnp.logical_not(sends_via))(pieces[p][n].start)
+                else:
+                    pieces[p][n].start()
+
+    def send_via():
+        if detour:
+            @pl.when(sends_via)
+            def _():
+                for copy in via:
+                    copy.start()
+
+    def send_onward():
+        if detour:
+            @pl.when(carries)
+            def _():
+                remote(count_ref, count_ref, via_sem.at[0], via_sem.at[0], (gx, gz)).wait_recv()
+                for copy in onward:
+                    copy.start()
 
     pltpu.make_async_copy(vel_ref.at[:, 0:4], pad.at[:, 0:4, 0:nz], load_sem.at[0]).wait()
-    pl.semaphore_wait(barrier, 4)
-    send(*EDGES, *NEAR)
+    pl.semaphore_wait(barrier, 3 + behind.astype(jnp.int32))
+
+    @pl.when(jnp.logical_not(ahead))
+    def _():
+        signal(wrap_sem, along_x(1))
+
+    send(*EDGES, *NEAR, sides=(1,))
+
+    @pl.when(behind)
+    def _():
+        send(*EDGES, *NEAR, sides=(0,))
+
     loads[2].wait()
     k_up.start()
     k_down.start()
@@ -163,7 +208,6 @@
     def learn():
         next(steps, None)
 
-    learn()
     sums[...] = jnp.zeros_like(sums)
     gap_load.wait()
     span = gap_ref[:, 0:ny] + gap_ref[:, 1:ny + 1]
@@ -280,14 +324,23 @@
             return carry
         lax.fori_loop(lo, hi, step, 0)
 
+
+    @pl.when(jnp.logical_not(behind))
+    def _():
+        pl.semaphore_wait(wrap_sem, 1)
+        send(*EDGES, *NEAR, sides=(0,))
+
+    learn()
     wait_for(4 * nx, kr_sem)
     over(3, nx + 1, first)
     learn()
+    send_via()
     smooth_row(2)
     smooth_row(nx + 1)
     over(4, nx, second)
     send(*far(0))
     send(*far(1))
+    send(*far(2))
     wait_for(16, xr_sem.at[0])
     relayed = []
     for p in range(2):
@@ -302,9 +355,9 @@
             body(p, sides[p])
 
     wait_for(2 * (nz - 4), xr_sem.at[1])
-    send(*far(2))
     learn()
     wait_for(16, cr_sem)
+    send_onward()
 
     def ready(p, rows):
         halo, edge = rows["halo"], rows["edge"]
@@ -385,6 +438,10 @@
     block = pad.at[:, 0:4, 0:nz]
     remote(block, block, xs_sem, xs_sem, (gx, gz)).wait_send()
     wait_for(16, cs_sem)
+    if detour:
+        @pl.when(carries)
+        def _():
+            remote(count_ref, count_ref, via_sem.at[1], via_sem.at[1], (gx, gz)).wait_send()
     for n, (_, _, count) in enumerate(rounds):
         acc = accs[n].at[:, 0:count]
         remote(acc, acc, as_sem.at[n], as_sem.at[n], (gx, gz)).wait_send()
@@ -423,9 +480,10 @@
             pltpu.VMEM((8, ny), f32),
             pltpu.VMEM((2, 8, ny), f32),
             tuple(pltpu.VMEM((ny // LANES, n, 2, LANES), f32) for n in members),
+            pltpu.VMEM((3, 1, nz, LANES), f32), pltpu.VMEM((3 * (nz - 4) // 4, 4, LANES), f32),
             pltpu.VMEM((1, ny + 1), f32), dma,
             dma((2,)), dma, dma((2 + ny // LANES,)), dma, dma, dma, dma,
-            flag((max(len(doublings(gxn)), 1),)), flag((max(len(doublings(gzn)), 1),)), flag,
+            flag((max(len(doublings(gxn)), 1),)), flag((max(len(doublings(gzn)), 1),)), flag, flag, dma((2,)),
             dma((len(members),)), dma((len(members), ny // LANES)),
         ],
         compiler_params=pltpu.CompilerParams(

time: 26.2 us -> 25.7 us (0.981)
  Pallas kernels: 25.4 us -> 24.9 us
    pallas_call x1, Pallas kernels: 24.4 us -> 23.8 us  [per_device(): pl.pallas_call(functools.partial(kernel, gxn, gzn, cells), out_shape=(hel...]
where the time goes in v6:
time: 25.7 us; the launch traced here: 25.5 us
  Pallas kernels  24.9 us (97%)
  between operations  0.64 us (2%)
    pallas_call x1, Pallas kernels, per_device(): pl.pallas_call(functools.partial(kernel, gxn, gzn, cells), out_shape=(hel...  23.8 us
    pallas_call x1, Pallas kernels, per_device(): pl.pallas_call(finish, out_shape=(field, field, field, jax.ShapeDtypeStru...  1.04 us

profile of v6, /device:TPU:0, one launch (start us, length us, event | category | flops | bytes accessed | tf_op | source)
XLA Modules:
  0.0 25.5 jit_solution(10581477745246259072)
XLA Ops:
  0.6 23.8 %shard_map.57 = (f32[8,32,384]{2,1,0:T(8,128)S(1)}, f32[8,32,384]{2,1,0:T(8,128)S(1)}, f32[8,32,384]{2,1,0:T(8,128)S(1)}, f32[2,384]{1,0:T(2,128)S(1)}) custom-call(f32[1,385]{1,0:T(1,128)} %bitcast.1, f32[3,8,32,384]{3,2,1,0:T(8,128)} %vel_ref.1), custom_call_target="tpu_custom_call" | custom-call | tf_op jit(solution)/shard_map/pallas_call | solution.py:463
  24.5 1.0 %shard_map.58 = (f32[8,32,384]{2,1,0:T(8,128)}, f32[8,32,384]{2,1,0:T(8,128)}, f32[8,32,384]{2,1,0:T(8,128)}, f32[384]{0:T(512)}) custom-call(f32[8,32,384]{2,1,0:T(8,128)S(1)} %get-tuple-element.8.size_ref, f32[8,32,384]{2,1,0:T(8,128)S(1)} %get-tuple-element.9.lm_ref, f32[8,32,384]{2,1,0:T(8,128)S(1)} %get-tuple-element.10.mm_ref, ...), custom_call_target="tpu_custom_call" | custom-call | tf_op jit(solution)/shard_map/pallas_call | solution.py:492

commit v7 on v6

--- a/solution.py
+++ b/solution.py
@@ -338,9 +338,6 @@
     smooth_row(2)
     smooth_row(nx + 1)
     over(4, nx, second)
-    send(*far(0))
-    send(*far(1))
-    send(*far(2))
     wait_for(16, xr_sem.at[0])
     relayed = []
     for p in range(2):
@@ -349,6 +346,9 @@
             relayed.append(remote(pad.at[:, rows, pl.ds(src, 2)], pad.at[:, rows, pl.ds(dst, 2)], cs_sem, cr_sem, device))
     for copy in relayed:
         copy.start()
+    send(*far(0))
+    send(*far(1))
+    send(*far(2))
 
     def both(body):
         for p in range(2):
@@ -357,7 +357,6 @@
     wait_for(2 * (nz - 4), xr_sem.at[1])
     learn()
     wait_for(16, cr_sem)
-    send_onward()
 
     def ready(p, rows):
         halo, edge = rows["halo"], rows["edge"]
@@ -385,6 +384,7 @@
                 rest_ref[p, n, :, cols] = zstress[n, rows["inner"], :, cols] + 2.0 * zstress[n, edge, :, cols]
 
     ready(0, sides[0])
+    send_onward()
     ready(1, sides[1])
     for _ in steps:
         pass

time: 25.7 us -> 25.7 us (level)
  no operation moved by 1% of the time
where the time goes in v7:
time: 25.7 us; the launch traced here: 25.5 us
  Pallas kernels  24.9 us (97%)
  between operations  0.64 us (2%)
    pallas_call x1, Pallas kernels, per_device(): pl.pallas_call(functools.partial(kernel, gxn, gzn, cells), out_shape=(hel...  23.8 us
    pallas_call x1, Pallas kernels, per_device(): pl.pallas_call(finish, out_shape=(field, field, field, jax.ShapeDtypeStru...  1.04 us

profile of v7, /device:TPU:0, one launch (start us, length us, event | category | flops | bytes accessed | tf_op | source)
XLA Modules:
  0.0 25.5 jit_solution(15287552941915400053)
XLA Ops:
  0.6 23.8 %shard_map.57 = (f32[8,32,384]{2,1,0:T(8,128)S(1)}, f32[8,32,384]{2,1,0:T(8,128)S(1)}, f32[8,32,384]{2,1,0:T(8,128)S(1)}, f32[2,384]{1,0:T(2,128)S(1)}) custom-call(f32[1,385]{1,0:T(1,128)} %bitcast.1, f32[3,8,32,384]{3,2,1,0:T(8,128)} %vel_ref.1), custom_call_target="tpu_custom_call" | custom-call | tf_op jit(solution)/shard_map/pallas_call | solution.py:463
  24.5 1.0 %shard_map.58 = (f32[8,32,384]{2,1,0:T(8,128)}, f32[8,32,384]{2,1,0:T(8,128)}, f32[8,32,384]{2,1,0:T(8,128)}, f32[384]{0:T(512)}) custom-call(f32[8,32,384]{2,1,0:T(8,128)S(1)} %get-tuple-element.8.size_ref, f32[8,32,384]{2,1,0:T(8,128)S(1)} %get-tuple-element.9.lm_ref, f32[8,32,384]{2,1,0:T(8,128)S(1)} %get-tuple-element.10.mm_ref, ...), custom_call_target="tpu_custom_call" | custom-call | tf_op jit(solution)/shard_map/pallas_call | solution.py:492
